TPU v7x, 512 devices: a whole 4x8x8 slice. The times are simulated.
512 devices in a mesh: leaf: 512 (over x, y, z, core).
Axes of the slice: x: 4, y: 8, z: 8, core: 2. Of those that a mesh axis runs over, the one named last changes fastest.
Arguments:
- vectors: float32 [16, 2097152], P(None, 'leaf'), may hold values from -6 to 6
- morton_order: int32 [512, 4096], P('leaf'), may hold values from 0 to 4095, each once within a row
- leaf_sizes: int32 [512, 32], P('leaf'), may hold values from 1 to 256, 4096 in all within a row
- leaf_basis: bfloat16 [32, 2097152], P(None, 'leaf'), may hold values from -0.5 to 0.5
- leaf_transfer: bfloat16 [16384, 1024], P('leaf'), may hold values from -0.75 to 0.75
- mid_transfer: bfloat16 [2048, 1024], P('leaf'), may hold values from -1 to 1
- root_transfer: bfloat16 [512, 1024], P('leaf'), may hold values from -0.75 to 0.75
- leaf_pairs: int32 [2, 32768], P(None, 'leaf'), may hold values from 0 to 31, as said below
- leaf_coupling: bfloat16 [32768, 1024], P('leaf'), may hold values from -0.5 to 0.5
- dev_partner: int32 [512, 128], P('leaf'), may hold values from -1 to 511, as said below
- dev_coupling: bfloat16 [65536, 1024], P('leaf'), may hold values from -0.25 to 0.25
- grp_partner: int32 [512, 4], P('leaf'), may hold values from 0 to 63, as said below
- grp_coupling: bfloat16 [2048, 1024], P('leaf'), may hold values from -0.5 to 0.5
Outputs:
- far_field: float32 [16, 2097152], P(None, 'leaf')
Inputs may be any that keep to these rules, and one draw needn't show every extreme that they name: `morton_order`: each row is a permutation of 0 to 4095. `leaf_pairs`: the two leaves of a pair differ. `dev_partner`: live entries of a row come first, are distinct and never the row's own subtree; an unordered pair of subtrees appears in at most one slot of all rows; some row has all 128 slots live. `grp_partner`: never the device's own group.
All inputs are finite; a program needn't handle non-finite values.
Results may differ from a plain program's by a relative error of at most 0.014.
Values may be sent and summed in bfloat16 or wider, within the bound.
A program may use at most 64 MiB of HBM per device.

v0:
```python
import jax
import jax.numpy as jnp
from jax import lax
from jax.sharding import Mesh
from jax.sharding import PartitionSpec as P

LEAF = 256
LEAF_AXES = ("leaf_0", "leaf_1", "leaf_2", "leaf_3")


highest = lax.Precision.HIGHEST


def from_everyone(array, axis):
    peers = lax.axis_size(axis)
    return lax.all_to_all(
        jnp.broadcast_to(array[None], (peers, *array.shape)), axis, 0, 0, tiled=True
    )


def in_order(parts, dim):
    dims = list(parts.shape[1:])
    dims[dim] *= parts.shape[0]
    return jnp.moveaxis(parts, 0, dim).reshape(dims)


def gathered_by_axis(array, axes, dim):
    far, near = axes
    parts = from_everyone(from_everyone(array, near), far)
    return in_order(parts.reshape(-1, *array.shape), dim)


def in_one_piece(arrays, axis, dim, along):
    ends, at = ([], 0)
    for a in arrays[:-1]:
        at += a.shape[along]
        ends.append(at)
    both = jnp.concatenate(arrays, axis=along)
    return tuple(jnp.split(gathered_by_axis(both, axis, dim), ends, axis=along))


def split_up(array, dim, peers):
    dims = array.shape
    parts = array.reshape(*dims[:dim], peers, dims[dim] // peers, *dims[dim + 1 :])
    return jnp.moveaxis(parts, dim, 0)


def sum_at_owner(array, axis, dim):
    peers = lax.axis_size(axis)
    parts = lax.all_to_all(split_up(array, dim, peers), axis, 0, 0, tiled=True)
    return jnp.sum(parts, axis=0)


def summed_rows(array, axes, dim):
    far, near = axes
    own = sum_at_owner(split_up(array, dim, lax.axis_size(far)), near, dim + 1)
    return jnp.sum(lax.all_to_all(own, far, 0, 0, tiled=True), axis=0)


def windows(sizes, total):
    starts = jnp.cumsum(sizes) - sizes
    offset = jnp.arange(LEAF, dtype=jnp.int32)
    places = starts[:, None] + offset[None, :]
    inside = offset[None, :] < sizes[:, None]
    return (jnp.minimum(places, total - 1), inside)


def body(
    vectors,
    morton_order,
    leaf_sizes,
    leaf_basis,
    leaf_transfer,
    mid_transfer,
    root_transfer,
    leaf_pairs,
    leaf_coupling,
    dev_partner,
    dev_coupling,
    grp_partner,
    grp_coupling,
):
    basis_rank = leaf_basis.shape[0]
    count_vec = vectors.shape[0]
    points = vectors.shape[1]
    leaves = leaf_sizes.shape[1]
    middle = mid_transfer.shape[0]
    row_width = basis_rank * count_vec
    subtrees = lax.axis_size(LEAF_AXES)
    groups = subtrees // 8
    self_id = lax.axis_index(LEAF_AXES)
    own_group = self_id // 8
    morton = morton_order[0]
    places, inside = windows(leaf_sizes[0], points)
    sorted_vec = vectors[:, morton].astype(jnp.bfloat16)
    basis_win = leaf_basis[:, places]
    vec_win = jnp.where(inside[None], sorted_vec[:, places], jnp.zeros((), jnp.bfloat16))
    leaf_coeff = jnp.einsum(
        "rls,vls->lrv", basis_win, vec_win, preferred_element_type=jnp.float32
    ).astype(jnp.bfloat16)
    leaf_maps = leaf_transfer.reshape(leaves, basis_rank, basis_rank)
    mid_maps = mid_transfer.reshape(middle, basis_rank, basis_rank)
    root_map = root_transfer.reshape(basis_rank, basis_rank)
    child = jnp.einsum("lij,liv->ljv", leaf_maps, leaf_coeff, preferred_element_type=jnp.float32)
    mid_coeff = child.reshape(middle, 8, basis_rank, count_vec).sum(1).astype(jnp.bfloat16)
    root_coeff = jnp.einsum(
        "mij,miv->jv", mid_maps, mid_coeff, preferred_element_type=jnp.float32
    ).astype(jnp.bfloat16)
    group_term = jnp.einsum(
        "ij,iv->jv", root_map, root_coeff, preferred_element_type=jnp.float32
    ).astype(jnp.bfloat16)
    dev_blocks = dev_coupling.reshape(-1, basis_rank, basis_rank)
    partner = dev_partner[0]
    is_live = partner >= 0
    sent_back = jnp.einsum(
        "cij,iv->cjv", dev_blocks, root_coeff, preferred_element_type=jnp.float32
    ).reshape(-1, row_width)
    sent_back = jnp.where(is_live[:, None], sent_back, 0.0)
    every = jnp.arange(subtrees, dtype=jnp.int32)
    own_flat = root_coeff.reshape(1, row_width)
    term_flat = group_term.reshape(1, row_width)
    coeff_all, term_all = in_one_piece(
        (own_flat, term_flat), (("leaf_0", "leaf_1"), ("leaf_2", "leaf_3")), 0, 1
    )
    row_count = coeff_all.shape[0]
    here_ids = jnp.arange(row_count, dtype=jnp.int32)
    picker = (partner[:, None] == here_ids[None, :]).astype(jnp.bfloat16)
    chosen = jnp.dot(picker, coeff_all, preferred_element_type=jnp.float32).astype(jnp.bfloat16)
    chosen = chosen.reshape(-1, basis_rank, count_vec)
    near_sum = jnp.einsum("cij,cjv->iv", dev_blocks, chosen, preferred_element_type=jnp.float32)
    member = ((here_ids // 8)[None, :] == jnp.arange(groups, dtype=jnp.int32)[:, None]).astype(
        jnp.bfloat16
    )
    group_sum = jnp.dot(member, term_all, preferred_element_type=jnp.float32)
    near_sum, group_sum = (near_sum, group_sum)
    group_coeff = group_sum.astype(jnp.bfloat16)
    grp_blocks = grp_coupling.reshape(-1, basis_rank, basis_rank)
    group_hot = (grp_partner[0][:, None] == jnp.arange(groups, dtype=jnp.int32)[None, :]).astype(
        jnp.bfloat16
    )
    far_coeff = jnp.dot(group_hot, group_coeff, preferred_element_type=jnp.float32).astype(
        jnp.bfloat16
    )
    far_coeff = far_coeff.reshape(-1, basis_rank, count_vec)
    home_coeff = lax.dynamic_slice_in_dim(group_coeff, own_group, 1, 0).reshape(
        basis_rank, count_vec
    )
    to_own = jnp.einsum(
        "cij,cjv->iv", grp_blocks, far_coeff, preferred_element_type=jnp.float32
    ).reshape(1, row_width)
    to_far = jnp.einsum(
        "cij,iv->cjv", grp_blocks, home_coeff, preferred_element_type=jnp.float32
    ).reshape(-1, row_width)
    self_hot = (jnp.arange(groups, dtype=jnp.int32) == own_group).astype(jnp.float32)[:, None]
    group_rows = self_hot * to_own + jnp.dot(
        group_hot.astype(jnp.float32).T, to_far, precision=highest
    )
    partner_hot = (partner[:, None] == every[None, :]).astype(jnp.float32)
    dev_buffer = jnp.dot(partner_hot.T, sent_back, precision=highest)
    widened = jnp.concatenate([dev_buffer, jnp.repeat(group_rows, 8, axis=0)], axis=1)
    returns = summed_rows(widened, (("leaf_0", "leaf_1"), ("leaf_2", "leaf_3")), 0)
    dev_back = returns[:, :row_width]
    group_here = returns[:, row_width:]
    root_far = near_sum + dev_back.reshape(basis_rank, count_vec)
    group_far = group_here.reshape(basis_rank, count_vec).astype(jnp.bfloat16)
    from_group = jnp.dot(root_map, group_far, preferred_element_type=jnp.float32)
    root_total = (root_far + from_group).astype(jnp.bfloat16)
    mid_total = jnp.einsum(
        "mij,jv->miv", mid_maps, root_total, preferred_element_type=jnp.float32
    ).astype(jnp.bfloat16)
    leaf_blocks = leaf_coupling.reshape(-1, basis_rank, basis_rank)
    leaf_ids = jnp.arange(leaves, dtype=jnp.int32)
    first_hot = (leaf_pairs[0][:, None] == leaf_ids[None, :]).astype(jnp.bfloat16)
    second_hot = (leaf_pairs[1][:, None] == leaf_ids[None, :]).astype(jnp.bfloat16)
    flat_coeff = leaf_coeff.reshape(leaves, row_width)
    from_second = jnp.dot(second_hot, flat_coeff, preferred_element_type=jnp.float32).astype(
        jnp.bfloat16
    )
    from_first = jnp.dot(first_hot, flat_coeff, preferred_element_type=jnp.float32).astype(
        jnp.bfloat16
    )
    forward = jnp.einsum(
        "pij,pjv->piv",
        leaf_blocks,
        from_second.reshape(-1, basis_rank, count_vec),
        preferred_element_type=jnp.float32,
    )
    backward = jnp.einsum(
        "pij,piv->pjv",
        leaf_blocks,
        from_first.reshape(-1, basis_rank, count_vec),
        preferred_element_type=jnp.float32,
    )
    leaf_far = jnp.dot(
        first_hot.astype(jnp.float32).T, forward.reshape(-1, row_width), precision=highest
    )
    leaf_far = leaf_far + jnp.dot(
        second_hot.astype(jnp.float32).T, backward.reshape(-1, row_width), precision=highest
    )
    parent = jnp.repeat(mid_total, 8, axis=0)
    leaf_down = jnp.einsum("lij,ljv->liv", leaf_maps, parent, preferred_element_type=jnp.float32)
    leaf_total = (leaf_down + leaf_far.reshape(leaves, basis_rank, count_vec)).astype(jnp.bfloat16)
    out_win = jnp.einsum("rls,lrv->vls", basis_win, leaf_total, preferred_element_type=jnp.float32)
    out_win = jnp.where(inside[None], out_win, 0.0)
    sorted_out = jnp.zeros((count_vec, points), jnp.float32).at[:, places].add(out_win)
    return jnp.zeros((count_vec, points), jnp.float32).at[:, morton].set(sorted_out)


def solution(mesh):
    split = Mesh(mesh.devices.reshape(4, 8, 8, 2), ("leaf_0", "leaf_1", "leaf_2", "leaf_3"))
    in_specs = (
        P(None, LEAF_AXES),
        P(LEAF_AXES, None),
        P(LEAF_AXES, None),
        P(None, LEAF_AXES),
        P(LEAF_AXES, None),
        P(LEAF_AXES, None),
        P(LEAF_AXES, None),
        P(None, LEAF_AXES),
        P(LEAF_AXES, None),
        P(LEAF_AXES, None),
        P(LEAF_AXES, None),
        P(LEAF_AXES, None),
        P(LEAF_AXES, None),
    )
    out_specs = P(None, LEAF_AXES)
    return jax.shard_map(body, mesh=split, in_specs=in_specs, out_specs=out_specs, check_vma=False)
```

profile of v0, /device:TPU:1, one launch (start us, length us, event | category | flops | bytes accessed | tf_op | source)
XLA Modules:
  0.0 270.3 jit_solution(12513471756193571838)
XLA Ops:
  0.0 0.7 reduce.3
  0.8 0.7 iota_compare_fusion.8
  1.5 0.7 compare_select_fusion
  2.3 0.7 copy.59
  3.2 0.7 bitcast_subtract_fusion
  4.0 0.6 copy-done.9
  4.6 0.8 reshape.260
  5.4 1.1 reshape.258
  6.5 1.4 copy.62
  7.9 12.1 %gather_fusion.1 = bf16[4096,16]{1,0:T(8,128)(2,1)S(1)} fusion(bf16[16,4096]{0,1:T(8,128)(2,1)S(1)} %copy.62, s32[4096]{0:T(1024)S(1)} %broadcast_clamp_fusion.1), kind=kCustom, calls=%fused_computation.1 | custom fusion | bytes 278528 | tf_op jit(solution)/shard_map/gather | solution.py:95
  20.0 24.0 %gather_fusion.2 = bf16[8192,16]{1,0:T(8,128)(2,1)S(1)} fusion(bf16[16,4096]{0,1:T(8,128)(2,1)S(1)} %bitcast.145, s32[8192]{0:T(1024)S(1)} %broadcast_clamp_fusion), kind=kCustom, calls=%fused_computation.2 | custom fusion | bytes 557056 | tf_op jit(solution)/shard_map/gather | solution.py:97
  44.1 1.4 copy.63
  45.5 1.4 copy.60
  47.0 24.0 %gather_fusion = bf16[8192,32]{1,0:T(8,128)(2,1)S(1)} fusion(bf16[32,4096]{0,1:T(8,128)(2,1)S(1)} %copy.60, s32[8192]{0:T(1024)S(1)} %broadcast_clamp_fusion), kind=kCustom, calls=%fused_computation | custom fusion | bytes 1081344 | tf_op jit(solution)/shard_map/gather | solution.py:96
  71.0 0.8 copy.61
  72.0 0.2 convolution_convert_fusion.1
  73.2 0.5 broadcast.198
  73.7 0.8 reduce.14
  74.6 19.0 %all_to_all.20 = bf16[16,2,512]{2,1,0:T(2,128)(2,1)S(1)} all-to-all(bf16[16,2,512]{2,1,0:T(2,128)(2,1)S(1)} %reshape.345), channel_id=1, replica_groups=mesh['leaf_0'=4,'leaf_1'=8,'leaf_2'=8,'leaf_3'=2] {'leaf_2','leaf_3'}, dimensions={0} | all-to-all | bytes 65536 | tf_op jit(solution)/shard_map/all_to_all | solution.py:16
  93.6 1.1 broadcast_in_dim.83
  94.8 9.7 %all-to-all-start.1 = ((bf16[32,16,1,1024]{3,1,2,0:T(8,128)(2,1)}), bf16[32,16,1,1024]{3,1,2,0:T(8,128)(2,1)S(1)}, u32[]{:S(2)}, u32[]{:S(2)}) async-start(bf16[32,16,1,1024]{3,1,2,0:T(8,128)(2,1)} %broadcast_in_dim.83), calls=%async_computation.1 | async-start | bytes 2097152 | tf_op jit(solution)/shard_map/all_to_all | solution.py:16
  105.0 0.6 convolution_bitcast_fusion
  105.7 24.0 %all-to-all-done.1 = bf16[32,16,1,1024]{3,1,2,0:T(8,128)(2,1)S(1)} async-done(((bf16[32,16,1,1024]{3,1,2,0:T(8,128)(2,1)}), bf16[32,16,1,1024]{3,1,2,0:T(8,128)(2,1)S(1)}, u32[]{:S(2)}, u32[]{:S(2)}) %all-to-all-start.1) | async-done | bytes 1048608 | tf_op jit(solution)/shard_map/all_to_all | solution.py:16
  131.0 0.3 convolution_add_fusion
  131.6 2.6 copy.75
  134.2 8.0 %all-to-all-start.2 = ((f32[16,32,1,1024]{3,1,2,0:T(8,128)}), f32[16,32,1,1024]{3,1,2,0:T(8,128)S(1)}, u32[]{:S(2)}, u32[]{:S(2)}) async-start(f32[16,32,1,1024]{3,1,2,0:T(8,128)} %copy.75), calls=%async_computation.2 | async-start | bytes 4194304 | tf_op jit(solution)/shard_map/all_to_all | solution.py:50
  142.4 0.8 copy.79
  143.2 1.7 copy.81
  145.3 0.2 convolution_convert_fusion.3
  145.7 1.0 copy.84
  146.7 0.3 copy.80
  147.0 2.0 convolution_bitcast_fusion.1
  149.0 2.0 copy.86
  151.0 1.2 convolution_bitcast_fusion.2
  152.2 1.4 copy.82
  153.6 0.3 fusion.33
  153.9 37.4 %all-to-all-done.2 = f32[16,32,1,1024]{3,1,2,0:T(8,128)S(1)} async-done(((f32[16,32,1,1024]{3,1,2,0:T(8,128)}), f32[16,32,1,1024]{3,1,2,0:T(8,128)S(1)}, u32[]{:S(2)}, u32[]{:S(2)}) %all-to-all-start.2) | async-done | bytes 2097184 | tf_op jit(solution)/shard_map/all_to_all | solution.py:50
  191.4 0.7 reduce_sum.33
  192.1 5.0 %all-to-all-start.3 = ((f32[32,1,1024]{2,1,0:T(1,128)}), f32[32,1,1024]{2,1,0:T(1,128)S(1)}, u32[]{:S(2)}, u32[]{:S(2)}) async-start(f32[32,1,1024]{2,1,0:T(1,128)} %reduce_sum.33), calls=%async_computation.3 | async-start | bytes 262144 | tf_op jit(solution)/shard_map/all_to_all | solution.py:57
  197.2 0.3 convolution_add_fusion.1
  197.9 1.3 convolution_convert_fusion
  199.3 6.8 %all-to-all-done.3 = f32[32,1,1024]{2,1,0:T(1,128)S(1)} async-done(((f32[32,1,1024]{2,1,0:T(1,128)}), f32[32,1,1024]{2,1,0:T(1,128)S(1)}, u32[]{:S(2)}, u32[]{:S(2)}) %all-to-all-start.3) | async-done | bytes 131104 | tf_op jit(solution)/shard_map/all_to_all | solution.py:57
  206.7 0.3 fusion.5
  207.1 0.4 fusion.2
  207.4 2.6 copy.97
  210.0 45.2 %scatter_custom_fusion = f32[16,4096]{0,1:T(8,128)S(1)} fusion(s32[8192]{0:T(1024)} %bitcast.167, f32[8192,16]{1,0:T(8,128)} %bitcast.146, f32[]{:T(128)} %constant.53.clone.1), kind=kCustom, calls=%fused_computation.41 | custom fusion | flops 131072 | bytes 262656 | tf_op jit(solution)/shard_map/scatter-add | solution.py:205
  255.2 12.2 %scatter_custom_fusion.1 = f32[16,4096]{0,1:T(8,128)} fusion(s32[4096]{0:T(1024)} %bitcast.170, f32[16,4096]{0,1:T(8,128)S(1)} %scatter_custom_fusion, f32[]{:T(128)} %constant.53.clone.1), kind=kCustom, calls=%fused_computation.6 | custom fusion | bytes 524800 | tf_op jit(solution)/shard_map/scatter | solution.py:206
  267.4 2.9 %copy.91 = f32[16,4096]{1,0:T(8,128)} copy(f32[16,4096]{0,1:T(8,128)} %scatter_custom_fusion.1) | data formatting | bytes 524288 | tf_op jit(solution)/shard_map/scatter | solution.py:206
  (95 shorter events, 5.5 us)
Async XLA Ops:
  2.3 41.8 %copy-start.10 = (s32[4096,1]{0,1:T(1,128)}, s32[4096,1]{0,1:T(1,128)S(1)}, u32[]{:S(2)}) copy-start(s32[4096,1]{0,1:T(1,128)S(1)} %compare_select_fusion) | copy-start | bytes 49156
  4.0 0.6 copy-start.9
  5.4 67.1 %copy-start.4 = (bf16[4,32,32]{2,1,0:T(8,128)(2,1)}, bf16[4,32,32]{2,1,0:T(8,128)(2,1)S(1)}, u32[]{:S(2)}) copy-start(bf16[4,32,32]{2,1,0:T(8,128)(2,1)S(1)} %reshape.260) | copy-start | bytes 24580
  71.0 1.0 copy-start.6
  72.0 22.8 %copy-start = (bf16[32,256,32]{1,2,0:T(8,128)(2,1)}, bf16[32,256,32]{1,2,0:T(8,128)(2,1)S(1)}, u32[]{:S(2)}) copy-start(bf16[32,256,32]{1,2,0:T(8,128)(2,1)S(1)} %copy.61) | copy-start | bytes 1572868
  72.2 32.3 %copy-start.11 = (bf16[4,1024]{1,0:T(4,128)(2,1)S(1)}, bf16[4,1024]{1,0:T(4,128)(2,1)}, u32[]{:S(2)}) copy-start(bf16[4,1024]{1,0:T(4,128)(2,1)} %param.25) | copy-start | bytes 24580
  72.2 32.4 %copy-start.7 = (bf16[128,1024]{1,0:T(8,128)(2,1)S(1)}, bf16[128,1024]{1,0:T(8,128)(2,1)}, u32[]{:S(2)}) copy-start(bf16[128,1024]{1,0:T(8,128)(2,1)} %param.23) | copy-start | bytes 786436
  74.6 30.2 %copy-start.17 = (s32[1,128]{1,0:T(1,128)S(1)}, s32[1,128]{1,0:T(1,128)}, u32[]{:S(2)}) copy-start(s32[1,128]{1,0:T(1,128)} %param.22) | copy-start | bytes 1540
  94.8 34.9 %all-to-all-start.1 = ((bf16[32,16,1,1024]{3,1,2,0:T(8,128)(2,1)}), bf16[32,16,1,1024]{3,1,2,0:T(8,128)(2,1)S(1)}, u32[]{:S(2)}, u32[]{:S(2)}) async-start(bf16[32,16,1,1024]{3,1,2,0:T(8,128)(2,1)} %broadcast_in_dim.83), calls=%async_computation.1 | async-start | bytes 2097152 | tf_op jit(solution)/shard_map/all_to_all | solution.py:16
  104.4 25.5 %copy-start.19 = (s32[1,4]{1,0:T(1,128)S(1)}, s32[1,4]{1,0:T(1,128)}, u32[]{:S(2)}) copy-start(s32[1,4]{1,0:T(1,128)} %param.24) | copy-start | bytes 52
  129.7 2.0 copy-start.3
  134.2 8.2 %copy-start.8 = (bf16[64,1024]{1,0:T(8,128)(2,1)S(1)}, bf16[64,1024]{1,0:T(8,128)(2,1)}, u32[]{:S(2)}) copy-start(bf16[64,1024]{1,0:T(8,128)(2,1)} %param.21) | copy-start | bytes 393220
  134.2 10.7 %copy-start.16 = (s32[2,64]{1,0:T(2,128)S(1)}, s32[2,64]{1,0:T(2,128)}, u32[]{:S(2)}) copy-start(s32[2,64]{1,0:T(2,128)} %param.20) | copy-start | bytes 1540
  134.2 57.1 %all-to-all-start.2 = ((f32[16,32,1,1024]{3,1,2,0:T(8,128)}), f32[16,32,1,1024]{3,1,2,0:T(8,128)S(1)}, u32[]{:S(2)}, u32[]{:S(2)}) async-start(f32[16,32,1,1024]{3,1,2,0:T(8,128)} %copy.75), calls=%async_computation.2 | async-start | bytes 4194304 | tf_op jit(solution)/shard_map/all_to_all | solution.py:50
  145.0 1.7 copy-start.12
  145.0 1.7 copy-start.14
  146.9 6.6 %copy-start.15 = (s32[64]{0:T(128)S(1)}, s32[64]{0:T(128)}, u32[]{:S(2)}) copy-start(s32[64]{0:T(128)} %copy-done.14) | copy-start | bytes 772
  152.2 45.0 %copy-start.2 = (f32[64,32,16]{0,2,1:T(8,128)S(1)}, f32[64,32,16]{0,2,1:T(8,128)}, u32[]{:S(2)}) copy-start(f32[64,32,16]{0,2,1:T(8,128)} %copy.86) | copy-start | bytes 393220
  152.2 45.0 %copy-start.13 = (s32[64]{0:T(128)S(1)}, s32[64]{0:T(128)}, u32[]{:S(2)}) copy-start(s32[64]{0:T(128)} %copy-done.12) | copy-start | bytes 772
  153.6 44.3 %copy-start.18 = (s32[1,128]{1,0:T(1,128)S(1)}, s32[1,128]{1,0:T(1,128)}, u32[]{:S(2)}) copy-start(s32[1,128]{1,0:T(1,128)} %param.22) | copy-start | bytes 1540
  191.4 15.3 %copy-start.5 = (bf16[4,32,32]{2,1,0:T(8,128)(2,1)S(1)}, bf16[4,32,32]{2,1,0:T(8,128)(2,1)}, u32[]{:S(2)}) copy-start(bf16[4,32,32]{2,1,0:T(8,128)(2,1)} %copy-done.4) | copy-start | bytes 24580
  191.4 15.6 %copy-start.1 = (bf16[32,256,32]{1,2,0:T(8,128)(2,1)S(1)}, bf16[32,256,32]{1,2,0:T(8,128)(2,1)}, u32[]{:S(2)}) copy-start(bf16[32,256,32]{1,2,0:T(8,128)(2,1)} %copy-done) | copy-start | bytes 1572868
  192.1 14.0 %all-to-all-start.3 = ((f32[32,1,1024]{2,1,0:T(1,128)}), f32[32,1,1024]{2,1,0:T(1,128)S(1)}, u32[]{:S(2)}, u32[]{:S(2)}) async-start(f32[32,1,1024]{2,1,0:T(1,128)} %reduce_sum.33), calls=%async_computation.3 | async-start | bytes 262144 | tf_op jit(solution)/shard_map/all_to_all | solution.py:57
where the time goes:
time: 271 us; the launch traced here: 270 us
  local copies, waits for them, and re-layouts  101 us (37%)
  waiting for transfers between devices  68.2 us (25%)
  other arithmetic  49.5 us (18%)
  starting transfers between devices  22.6 us (8%)
  blocking collectives  19 us (7%)
  matrix products  9.1 us (3%)
    scatter-add x1, other arithmetic, body(): jnp.zeros((count_vec, points), jnp.float32).at[:, places].add(out_win)  45.2 us
    all_to_all x1, waiting for transfers between devices, sum_at_owner(): parts = lax.all_to_all(split_up(array, dim, peers), axis, 0, 0, tiled=True)  37.4 us
    gather x2, local copies, waits for them, and re-layouts, body(): sorted_vec[:, places]  25.5 us
    gather x2, local copies, waits for them, and re-layouts, body(): basis_win = leaf_basis[:, places]  24.8 us
    all_to_all x1, waiting for transfers between devices, from_everyone(): lax.all_to_all(jnp.broadcast_to(array[None], (peers, *array.shape)), axis...  24 us
    all_to_all x1, blocking collectives, from_everyone(): lax.all_to_all(jnp.broadcast_to(array[None], (peers, *array.shape)), axis...  19 us
    scatter x2, local copies, waits for them, and re-layouts, body(): jnp.zeros((count_vec, points), jnp.float32).at[:, morton].set(sorted_out)  15.1 us
    gather x1, local copies, waits for them, and re-layouts, body(): sorted_vec = vectors[:, morton].astype(jnp.bfloat16)  12.1 us
  transfers between devices with their start and end apart: 3, of which 3 were waited for; matrix products, arithmetic and copies ran while one was open for 5% of the time, Pallas kernels for 0%

commit v1 on v0

--- a/solution.py
+++ b/solution.py
@@ -1,11 +1,180 @@
 import jax
 import jax.numpy as jnp
 from jax import lax
+from jax.experimental import pallas as pl
+from jax.experimental.pallas import tpu as pltpu
 from jax.sharding import Mesh
 from jax.sharding import PartitionSpec as P
 
 LEAF = 256
 LEAF_AXES = ("leaf_0", "leaf_1", "leaf_2", "leaf_3")
+
+
+F32, BF16, I32 = jnp.float32, jnp.bfloat16, jnp.int32
+NT = (((1,), (1,)), ((), ()))
+TN = (((0,), (0,)), ((), ()))
+
+
+def iota(shape, dim):
+    return lax.broadcasted_iota(I32, shape, dim)
+
+
+def dot(a, b, dims=(((1,), (0,)), ((), ()))):
+    return lax.dot_general(a, b, dims, preferred_element_type=F32)
+
+
+def hot(mask):
+    return jnp.where(mask, 1.0, 0.0).astype(BF16)
+
+
+def spread_row():
+    return hot(iota((32, 1024), 1) // 32 == iota((32, 1024), 0))
+
+
+def spread_col():
+    return hot(iota((32, 1024), 1) % 32 == iota((32, 1024), 0))
+
+
+def fold_first(x):
+    w = x[:, 0:128]
+    for q in range(1, 8):
+        w = w + x[:, q * 128 : (q + 1) * 128]
+    return (w[:, 0:32] + w[:, 32:64]) + (w[:, 64:96] + w[:, 96:128])
+
+
+def leaf_of(siz_ref, start, width):
+    sizes = siz_ref[...].astype(F32)
+    lower = iota((32, 32), 1) <= iota((32, 32), 0)
+    ends = jnp.sum(jnp.where(lower, jnp.broadcast_to(sizes, (32, 32)), 0.0), axis=1, keepdims=True)
+    pos = (iota((32, width), 1) + start).astype(F32)
+    return jnp.sum(jnp.where(pos >= ends, 1.0, 0.0), axis=0, keepdims=True)
+
+
+CH = 256
+
+
+def up_kernel(vec, mor, siz, bas, lt, mt, rt, lc_out, root_out, term_out, masked, lt32):
+    lt32[...] = lt[...].astype(F32)
+    vx = jnp.concatenate([vec[:, h * 256 : (h + 1) * 256] for h in range(16)], axis=0).astype(BF16)
+
+    def chunk(c, carry):
+        at = pl.multiple_of(c * CH, CH)
+        m = mor[:, pl.ds(at, CH)]
+        lo, hi = m & 255, m >> 8
+        pick = hot(iota((256, CH), 0) == lo)
+        wide = dot(vx, pick)
+        hib = jnp.broadcast_to(hi, (16, CH))
+        sv = wide[0:16]
+        for h in range(1, 16):
+            sv = jnp.where(hib == h, wide[h * 16 : (h + 1) * 16], sv)
+        leaf = jnp.broadcast_to(leaf_of(siz, at, CH), (16, CH)).astype(BF16)
+        svb = sv.astype(BF16)
+        for l in range(32):
+            masked[l * 16 : (l + 1) * 16, pl.ds(at, CH)] = jnp.where(leaf == l, svb, jnp.zeros((), BF16))
+        return carry
+
+    lax.fori_loop(0, 4096 // CH, chunk, 0)
+    lc = dot(masked[...], bas[...], NT).astype(BF16)
+    lc_out[...] = lc
+    erow = spread_row()
+    root = jnp.zeros((16, 1024), F32)
+    for m in range(4):
+        acc = jnp.zeros((16, 1024), F32)
+        x = dot(lc[m * 128 : (m + 1) * 128], erow)
+        for l in range(8):
+            acc = acc + x[l * 16 : (l + 1) * 16] * lt32[m * 8 + l : m * 8 + l + 1, :]
+        mid = fold_first(acc).astype(BF16)
+        root = root + dot(mid, erow) * mt[m : m + 1, :].astype(F32)
+    root = fold_first(root).astype(BF16)
+    root_out[...] = root
+    term_out[...] = fold_first(dot(root, erow) * rt[...].astype(F32)).astype(BF16)
+
+
+def pair_kernel(idx, lc, pairs, coup, far_out, s32, got, fwd, bwd):
+    s32[...] = coup[...].astype(F32)
+    erow, ecol = spread_row(), spread_col()
+    back = hot(iota((1024, 32), 0) // 32 == iota((1024, 32), 1))
+
+    def group(g, carry):
+        for which, e in ((1, ecol), (0, erow)):
+            for k in range(8):
+                b = idx[which, g * 8 + k]
+                got[k * 16 : (k + 1) * 16, :] = lc[pl.ds(pl.multiple_of(b * 16, 16), 16), :]
+            x = dot(got[...], e)
+            parts = [x[k * 16 : (k + 1) * 16] * s32[pl.ds(g * 8 + k, 1), :] for k in range(8)]
+            if which == 1:
+                y = dot(jnp.concatenate(parts, axis=0).astype(BF16), back)
+                fwd[pl.ds(pl.multiple_of(g * 128, 128), 128), :] = y.astype(BF16)
+            else:
+                y = jnp.concatenate([fold_first(t) for t in parts], axis=0)
+                bwd[pl.ds(pl.multiple_of(g * 128, 128), 128), :] = y.astype(BF16)
+        return carry
+
+    lax.fori_loop(0, 8, group, 0)
+    wide = hot(iota((64, 1024), 1) // 16 == iota((64, 1024), 0))
+    ids = dot(pairs[...].astype(F32).astype(BF16), wide)
+    same = iota((512, 1024), 0) % 16 == iota((512, 1024), 1) % 16
+    leaf = (iota((512, 1024), 0) // 16).astype(F32)
+    far_out[...] = dot(hot(same & (leaf == ids[0:1])), fwd[...]) + dot(hot(same & (leaf == ids[1:2])), bwd[...])
+
+
+def down_kernel(top, far, mor, siz, bas, lt, mt, out, scat):
+    erow, ecol = spread_row(), spread_col()
+    back = hot(iota((1024, 32), 0) // 32 == iota((1024, 32), 1))
+    xt = dot(top[...], ecol)
+    p = jnp.concatenate([xt * mt[m : m + 1, :].astype(F32) for m in range(4)], axis=0)
+    ph = p.astype(BF16)
+    pl_ = (p - ph.astype(F32)).astype(BF16)
+    mid = (dot(ph, back) + dot(pl_, back)).astype(BF16)
+    tots = []
+    for m in range(4):
+        x = dot(mid[m * 16 : (m + 1) * 16], ecol)
+        q = jnp.concatenate(
+            [x * lt[m * 8 + l : m * 8 + l + 1, :].astype(F32) for l in range(8)], axis=0
+        ).astype(BF16)
+        tots.append((dot(q, back) + far[m * 128 : (m + 1) * 128, :]).astype(BF16))
+    tot = jnp.concatenate(tots, axis=0)
+
+    def chunk(c, acc):
+        at = pl.multiple_of(c * CH, CH)
+        m = mor[:, pl.ds(at, CH)]
+        lo, hi = m & 255, m >> 8
+        pick = hot(iota((256, CH), 0) == lo)
+        wide = dot(tot, bas[:, pl.ds(at, CH)])
+        leaf = jnp.broadcast_to(leaf_of(siz, at, CH), (16, CH))
+        o = wide[0:16]
+        for l in range(1, 32):
+            o = jnp.where(leaf == l, wide[l * 16 : (l + 1) * 16], o)
+        ob = o.astype(BF16)
+        hib = jnp.broadcast_to(hi, (16, CH)).astype(F32).astype(BF16)
+        for h in range(16):
+            scat[h * 16 : (h + 1) * 16, :] = jnp.where(hib == h, ob, jnp.zeros((), BF16))
+        return acc + dot(scat[...], pick, NT)
+
+    acc = lax.fori_loop(0, 4096 // CH, chunk, jnp.zeros((256, 256), F32))
+    for h in range(16):
+        out[:, h * 256 : (h + 1) * 256] = acc[h * 16 : (h + 1) * 16]
+
+
+S = jax.ShapeDtypeStruct
+VM = pltpu.VMEM
+
+
+def up(vec, mor, siz, bas, lt, mt, rt):
+    return pl.pallas_call(up_kernel, out_shape=(S((512, 32), BF16), S((16, 32), BF16), S((16, 32), BF16)),
+        scratch_shapes=[VM((512, 4096), BF16), VM((32, 1024), F32)])(vec, mor, siz, bas, lt, mt, rt)
+
+
+def pairs_(idx, lc, coup):
+    vm = pl.BlockSpec(memory_space=pltpu.VMEM)
+    return pl.pallas_call(pair_kernel, out_shape=S((512, 32), F32),
+        in_specs=[pl.BlockSpec(memory_space=pltpu.SMEM), vm, vm, vm],
+        scratch_shapes=[VM((64, 1024), F32), VM((128, 32), BF16), VM((1024, 32), BF16), VM((1024, 32), BF16)])(idx, lc, idx, coup)
+
+
+def down(top, far, mor, siz, bas, lt, mt):
+    return pl.pallas_call(down_kernel, out_shape=S((16, 4096), F32),
+        scratch_shapes=[VM((256, CH), BF16)])(top, far, mor, siz, bas, lt, mt)
 
 
 highest = lax.Precision.HIGHEST
@@ -55,14 +224,6 @@
     far, near = axes
     own = sum_at_owner(split_up(array, dim, lax.axis_size(far)), near, dim + 1)
     return jnp.sum(lax.all_to_all(own, far, 0, 0, tiled=True), axis=0)
-
-
-def windows(sizes, total):
-    starts = jnp.cumsum(sizes) - sizes
-    offset = jnp.arange(LEAF, dtype=jnp.int32)
-    places = starts[:, None] + offset[None, :]
-    inside = offset[None, :] < sizes[:, None]
-    return (jnp.minimum(places, total - 1), inside)
 
 
 def body(
@@ -82,33 +243,18 @@
 ):
     basis_rank = leaf_basis.shape[0]
     count_vec = vectors.shape[0]
-    points = vectors.shape[1]
-    leaves = leaf_sizes.shape[1]
-    middle = mid_transfer.shape[0]
     row_width = basis_rank * count_vec
     subtrees = lax.axis_size(LEAF_AXES)
     groups = subtrees // 8
     self_id = lax.axis_index(LEAF_AXES)
     own_group = self_id // 8
-    morton = morton_order[0]
-    places, inside = windows(leaf_sizes[0], points)
-    sorted_vec = vectors[:, morton].astype(jnp.bfloat16)
-    basis_win = leaf_basis[:, places]
-    vec_win = jnp.where(inside[None], sorted_vec[:, places], jnp.zeros((), jnp.bfloat16))
-    leaf_coeff = jnp.einsum(
-        "rls,vls->lrv", basis_win, vec_win, preferred_element_type=jnp.float32
-    ).astype(jnp.bfloat16)
-    leaf_maps = leaf_transfer.reshape(leaves, basis_rank, basis_rank)
-    mid_maps = mid_transfer.reshape(middle, basis_rank, basis_rank)
+    lc, root_t, term_t = up(
+        vectors, morton_order, leaf_sizes, leaf_basis, leaf_transfer, mid_transfer, root_transfer
+    )
     root_map = root_transfer.reshape(basis_rank, basis_rank)
-    child = jnp.einsum("lij,liv->ljv", leaf_maps, leaf_coeff, preferred_element_type=jnp.float32)
-    mid_coeff = child.reshape(middle, 8, basis_rank, count_vec).sum(1).astype(jnp.bfloat16)
-    root_coeff = jnp.einsum(
-        "mij,miv->jv", mid_maps, mid_coeff, preferred_element_type=jnp.float32
-    ).astype(jnp.bfloat16)
-    group_term = jnp.einsum(
-        "ij,iv->jv", root_map, root_coeff, preferred_element_type=jnp.float32
-    ).astype(jnp.bfloat16)
+    root_coeff = root_t.T
+    group_term = term_t.T
+    far = pairs_(leaf_pairs, lc, leaf_coupling)
     dev_blocks = dev_coupling.reshape(-1, basis_rank, basis_rank)
     partner = dev_partner[0]
     is_live = partner >= 0
@@ -165,45 +311,9 @@
     group_far = group_here.reshape(basis_rank, count_vec).astype(jnp.bfloat16)
     from_group = jnp.dot(root_map, group_far, preferred_element_type=jnp.float32)
     root_total = (root_far + from_group).astype(jnp.bfloat16)
-    mid_total = jnp.einsum(
-        "mij,jv->miv", mid_maps, root_total, preferred_element_type=jnp.float32
-    ).astype(jnp.bfloat16)
-    leaf_blocks = leaf_coupling.reshape(-1, basis_rank, basis_rank)
-    leaf_ids = jnp.arange(leaves, dtype=jnp.int32)
-    first_hot = (leaf_pairs[0][:, None] == leaf_ids[None, :]).astype(jnp.bfloat16)
-    second_hot = (leaf_pairs[1][:, None] == leaf_ids[None, :]).astype(jnp.bfloat16)
-    flat_coeff = leaf_coeff.reshape(leaves, row_width)
-    from_second = jnp.dot(second_hot, flat_coeff, preferred_element_type=jnp.float32).astype(
-        jnp.bfloat16
-    )
-    from_first = jnp.dot(first_hot, flat_coeff, preferred_element_type=jnp.float32).astype(
-        jnp.bfloat16
-    )
-    forward = jnp.einsum(
-        "pij,pjv->piv",
-        leaf_blocks,
-        from_second.reshape(-1, basis_rank, count_vec),
-        preferred_element_type=jnp.float32,
-    )
-    backward = jnp.einsum(
-        "pij,piv->pjv",
-        leaf_blocks,
-        from_first.reshape(-1, basis_rank, count_vec),
-        preferred_element_type=jnp.float32,
-    )
-    leaf_far = jnp.dot(
-        first_hot.astype(jnp.float32).T, forward.reshape(-1, row_width), precision=highest
-    )
-    leaf_far = leaf_far + jnp.dot(
-        second_hot.astype(jnp.float32).T, backward.reshape(-1, row_width), precision=highest
-    )
-    parent = jnp.repeat(mid_total, 8, axis=0)
-    leaf_down = jnp.einsum("lij,ljv->liv", leaf_maps, parent, preferred_element_type=jnp.float32)
-    leaf_total = (leaf_down + leaf_far.reshape(leaves, basis_rank, count_vec)).astype(jnp.bfloat16)
-    out_win = jnp.einsum("rls,lrv->vls", basis_win, leaf_total, preferred_element_type=jnp.float32)
-    out_win = jnp.where(inside[None], out_win, 0.0)
-    sorted_out = jnp.zeros((count_vec, points), jnp.float32).at[:, places].add(out_win)
-    return jnp.zeros((count_vec, points), jnp.float32).at[:, morton].set(sorted_out)
+    return down(
+        root_total.T, far, morton_order, leaf_sizes, leaf_basis, leaf_transfer, mid_transfer
+    )
 
 
 def solution(mesh):

time: 271 us -> 156 us (0.58)
  local copies, waits for them, and re-layouts: 101 us -> 6.92 us
  blocking collectives: 19 us -> 76.8 us
  other arithmetic: 49.5 us -> 1.31 us
  waiting for transfers between devices: 68.2 us -> 26.5 us
  Pallas kernels: 0 us -> 26.6 us
  starting transfers between devices: 22.6 us -> 14.5 us
  matrix products: 9.1 us -> 3.14 us
    gather x5 -> x0, local copies, waits for them, and re-layouts: 62.5 us -> none  [the longest x2 25.5 us: body(): sorted_vec[:, places]]
    all_to_all x0 -> x1, blocking collectives: none -> 57.8 us  [sum_at_owner(): parts = lax.all_to_all(split_up(array, dim, peers), axis, 0, 0, tiled=True)]
    scatter-add x1 -> x0, other arithmetic: 45.2 us -> none  [body(): jnp.zeros((count_vec, points), jnp.float32).at[:, places].add(out_win)]
    all_to_all x1 -> x0, waiting for transfers between devices: 37.4 us -> none  [sum_at_owner(): parts = lax.all_to_all(split_up(array, dim, peers), axis, 0, 0, tiled=True)]
    pallas_call x0 -> x3, Pallas kernels: none -> 26.6 us  [the longest x1 10.3 us: down(): pl.pallas_call(down_kernel, out_shape=S((16, 4096), F32), scratch_shapes=...]
    scatter x2 -> x0, local copies, waits for them, and re-layouts: 15.1 us -> none  [body(): jnp.zeros((count_vec, points), jnp.float32).at[:, morton].set(sorted_out)]
    all_to_all x1 -> x0, starting transfers between devices: 7.96 us -> none  [sum_at_owner(): parts = lax.all_to_all(split_up(array, dim, peers), axis, 0, 0, tiled=True)]
    reshape x6 -> x0, local copies, waits for them, and re-layouts: 5.04 us -> none  [the longest x1 1.72 us: body(): leaf_blocks = leaf_coupling.reshape(-1, basis_rank, basis_rank)]
  transfers between devices with their start and end apart: 3 -> 2, of which waited for: 3 -> 2; matrix products, arithmetic and copies ran while one was open for 5% -> 1% of each run, Pallas kernels for 0% -> 5%
where the time goes in v1:
time: 156 us
  blocking collectives  76.8 us (49%)
  Pallas kernels  26.6 us (17%)
  waiting for transfers between devices  26.5 us (17%)
  starting transfers between devices  14.5 us (9%)
  local copies, waits for them, and re-layouts  6.92 us (4%)
  matrix products  3.14 us (2%)
    all_to_all x1, blocking collectives, sum_at_owner(): parts = lax.all_to_all(split_up(array, dim, peers), axis, 0, 0, tiled=True)  57.8 us
    all_to_all x1, waiting for transfers between devices, from_everyone(): lax.all_to_all(jnp.broadcast_to(array[None], (peers, *array.shape)), axis...  24 us
    all_to_all x1, blocking collectives, from_everyone(): lax.all_to_all(jnp.broadcast_to(array[None], (peers, *array.shape)), axis...  19 us
    pallas_call x1, Pallas kernels, down(): pl.pallas_call(down_kernel, out_shape=S((16, 4096), F32), scratch_shapes=...  10.3 us
    all_to_all x1, starting transfers between devices, from_everyone(): lax.all_to_all(jnp.broadcast_to(array[None], (peers, *array.shape)), axis...  9.67 us
    pallas_call x1, Pallas kernels, up(): pl.pallas_call(up_kernel, out_shape=(S((512, 32), BF16), S((16, 32), BF16...  9.17 us
    pallas_call x1, Pallas kernels, pairs_(): pl.pallas_call(pair_kernel, out_shape=S((512, 32), F32), in_specs=[pl.Blo...  7.07 us
    all_to_all x1, starting transfers between devices, summed_rows(): return jnp.sum(lax.all_to_all(own, far, 0, 0, tiled=True), axis=0)  4.84 us
  transfers between devices with their start and end apart: 2, of which 2 were waited for; matrix products, arithmetic and copies ran while one was open for 1% of the time, Pallas kernels for 5%

profile of v1, /device:TPU:1, one launch (start us, length us, event | category | flops | bytes accessed | tf_op | source)
XLA Modules:
  0.0 156.0 jit_solution(1544185768648211083)
XLA Ops:
  0.0 9.2 %shard_map.127 = (bf16[512,32]{1,0:T(8,128)(2,1)}, bf16[16,32]{1,0:T(8,128)(2,1)}, bf16[16,32]{1,0:T(8,128)(2,1)}) custom-call(f32[16,4096]{1,0:T(8,128)} %vec.1, s32[1,4096]{1,0:T(1,128)} %mor.3, s32[1,32]{1,0:T(1,128)} %siz.3, bf16[32,4096]{1,0:T(8,128)(2,1)} %bas.3, bf16[32,1024]{1,0:T(8,128)(2,1)} %lt.7, bf16[4,1024]{1,0:T(4,128)(2,1)} %mt.3, ...), custom_call_target="tpu_custom_call" | custom-call | tf_op jit(solution)/shard_map/pallas_call | solution.py:164
  9.2 0.8 copy.32
  9.9 0.1 reshape.100
  10.0 0.8 copy.31
  10.8 0.1 reshape.99
  11.0 0.6 broadcast.76
  11.5 0.9 reduce.13
  12.4 0.0 copy-start.4
  12.4 0.0 copy-start.1
  12.5 19.0 %all_to_all.20 = bf16[16,2,512]{2,1,0:T(2,128)(2,1)S(1)} all-to-all(bf16[16,2,512]{2,1,0:T(2,128)(2,1)S(1)} %reshape.125), channel_id=1, replica_groups=mesh['leaf_0'=4,'leaf_1'=8,'leaf_2'=8,'leaf_3'=2] {'leaf_2','leaf_3'}, dimensions={0} | all-to-all | bytes 65536 | tf_op jit(solution)/shard_map/all_to_all | solution.py:185
  31.5 1.1 broadcast_in_dim.41
  32.6 9.7 %all-to-all-start.1 = ((bf16[32,16,1,1024]{3,1,2,0:T(8,128)(2,1)}), bf16[32,16,1,1024]{3,1,2,0:T(8,128)(2,1)S(1)}, u32[]{:S(2)}, u32[]{:S(2)}) async-start(bf16[32,16,1,1024]{3,1,2,0:T(8,128)(2,1)} %broadcast_in_dim.41), calls=%async_computation.1 | async-start | bytes 2097152 | tf_op jit(solution)/shard_map/all_to_all | solution.py:185
  42.3 0.0 copy-start.5
  42.4 0.1 reshape.104
  42.5 0.2 copy.34
  42.7 0.2 convolution_select_fusion
  42.9 0.6 convolution_bitcast_fusion
  43.5 24.0 %all-to-all-done.1 = bf16[32,16,1,1024]{3,1,2,0:T(8,128)(2,1)S(1)} async-done(((bf16[32,16,1,1024]{3,1,2,0:T(8,128)(2,1)}), bf16[32,16,1,1024]{3,1,2,0:T(8,128)(2,1)S(1)}, u32[]{:S(2)}, u32[]{:S(2)}) %all-to-all-start.1) | async-done | bytes 1048608 | tf_op jit(solution)/shard_map/all_to_all | solution.py:185
  67.6 0.2 convolution_convert_fusion.1
  67.8 0.2 convolution_convert_fusion.2
  68.0 0.1 reshape.105
  68.1 0.1 reshape.103
  68.2 0.2 convolution_bitcast_fusion.1
  68.4 0.2 convolution_bitcast_fusion.3
  68.5 0.1 copy.39
  68.6 0.1 mul.28
  68.7 0.1 copy.41
  68.8 0.1 reshape.106
  68.9 0.3 convolution_add_fusion
  69.2 0.1 broadcast_in_dim.44
  69.3 0.2 maximum_bitcast_fusion
  69.5 1.2 copy.42
  70.7 57.8 %all_to_all.21 = f32[16,32,1,1024]{3,1,2,0:T(8,128)S(1)} all-to-all(f32[16,32,1,1024]{3,1,2,0:T(8,128)S(1)} %copy.42), channel_id=1, replica_groups=mesh['leaf_0'=4,'leaf_1'=8,'leaf_2'=8,'leaf_3'=2] {'leaf_2','leaf_3'}, dimensions={0} | all-to-all | bytes 4194304 | tf_op jit(solution)/shard_map/all_to_all | solution.py:219
  128.5 0.1 reduce_sum.22
  128.6 0.8 reduce_sum.23
  129.4 4.8 %all-to-all-start.3 = ((f32[32,1,1024]{2,1,0:T(1,128)}), f32[32,1,1024]{2,1,0:T(1,128)S(1)}, u32[]{:S(2)}, u32[]{:S(2)}) async-start(f32[32,1,1024]{2,1,0:T(1,128)} %reduce_sum.23), calls=%async_computation.3 | async-start | bytes 262144 | tf_op jit(solution)/shard_map/all_to_all | solution.py:226
  134.3 0.1 reshape.108
  134.4 7.1 %shard_map.128.far = f32[512,32]{1,0:T(8,128)} custom-call(s32[2,64]{1,0:T(2,128)} %pairs.1, bf16[512,32]{1,0:T(8,128)(2,1)} %get-tuple-element.10.lc, s32[2,64]{1,0:T(2,128)} %pairs.1, bf16[64,1024]{1,0:T(8,128)(2,1)} %coup.1), custom_call_target="tpu_custom_call" | custom-call | tf_op jit(solution)/shard_map/pallas_call | solution.py:170
  141.4 0.3 convolution_convert_fusion
  141.7 0.1 copy.33
  141.8 2.5 %all-to-all-done.3 = f32[32,1,1024]{2,1,0:T(1,128)S(1)} async-done(((f32[32,1,1024]{2,1,0:T(1,128)}), f32[32,1,1024]{2,1,0:T(1,128)S(1)}, u32[]{:S(2)}, u32[]{:S(2)}) %all-to-all-start.3) | async-done | bytes 131104 | tf_op jit(solution)/shard_map/all_to_all | solution.py:226
  144.3 0.1 reduce_sum.24
  144.4 0.1 convert_element_type.32
  144.5 0.1 reshape.107
  144.6 0.1 copy.43
  144.6 0.2 fusion.1
  144.9 0.8 fusion.3.top
  145.6 10.3 %shard_map.129 = f32[16,4096]{1,0:T(8,128)} custom-call(bf16[16,32]{1,0:T(8,128)(2,1)} %fusion.3.top, f32[512,32]{1,0:T(8,128)} %shard_map.128.far, s32[1,4096]{1,0:T(1,128)} %mor.3, s32[1,32]{1,0:T(1,128)} %siz.3, bf16[32,4096]{1,0:T(8,128)(2,1)} %bas.3, bf16[32,1024]{1,0:T(8,128)(2,1)} %lt.7, bf16[4,1024]{1,0:T(4,128)(2,1)} %mt.3), custom_call_target="tpu_custom_call" | custom-call | tf_op jit(solution)/shard_map/pallas_call | solution.py:176
  (22 shorter events, 0.3 us)
Async XLA Ops:
  0.0 42.4 %copy-start.3 = (bf16[4,1024]{1,0:T(4,128)(2,1)S(1)}, bf16[4,1024]{1,0:T(4,128)(2,1)}, u32[]{:S(2)}) copy-start(bf16[4,1024]{1,0:T(4,128)(2,1)} %param.25) | copy-start | bytes 24580
  0.0 42.5 %copy-start = (bf16[128,1024]{1,0:T(8,128)(2,1)S(1)}, bf16[128,1024]{1,0:T(8,128)(2,1)}, u32[]{:S(2)}) copy-start(bf16[128,1024]{1,0:T(8,128)(2,1)} %param.23) | copy-start | bytes 786436
  12.4 30.3 %copy-start.4 = (s32[1,128]{1,0:T(1,128)S(1)}, s32[1,128]{1,0:T(1,128)}, u32[]{:S(2)}) copy-start(s32[1,128]{1,0:T(1,128)} %param.22) | copy-start | bytes 1540
  12.4 30.3 %copy-start.1 = (bf16[16,32]{1,0:T(8,128)(2,1)S(1)}, bf16[16,32]{1,0:T(8,128)(2,1)}, u32[]{:S(2)}) copy-start(bf16[16,32]{1,0:T(8,128)(2,1)} %get-tuple-element.8) | copy-start | bytes 3076
  32.6 34.9 %all-to-all-start.1 = ((bf16[32,16,1,1024]{3,1,2,0:T(8,128)(2,1)}), bf16[32,16,1,1024]{3,1,2,0:T(8,128)(2,1)S(1)}, u32[]{:S(2)}, u32[]{:S(2)}) async-start(bf16[32,16,1,1024]{3,1,2,0:T(8,128)(2,1)} %broadcast_in_dim.41), calls=%async_computation.1 | async-start | bytes 2097152 | tf_op jit(solution)/shard_map/all_to_all | solution.py:185
  42.3 25.5 %copy-start.5 = (s32[1,4]{1,0:T(1,128)S(1)}, s32[1,4]{1,0:T(1,128)}, u32[]{:S(2)}) copy-start(s32[1,4]{1,0:T(1,128)} %param.24) | copy-start | bytes 52
  128.5 5.7 %copy-start.2 = (bf16[1,1024]{1,0:T(2,128)(2,1)S(1)}, bf16[1,1024]{1,0:T(2,128)(2,1)}, u32[]{:S(2)}) copy-start(bf16[1,1024]{1,0:T(2,128)(2,1)} %rt.1) | copy-start | bytes 6148
  129.4 14.9 %all-to-all-start.3 = ((f32[32,1,1024]{2,1,0:T(1,128)}), f32[32,1,1024]{2,1,0:T(1,128)S(1)}, u32[]{:S(2)}, u32[]{:S(2)}) async-start(f32[32,1,1024]{2,1,0:T(1,128)} %reduce_sum.23), calls=%async_computation.3 | async-start | bytes 262144 | tf_op jit(solution)/shard_map/all_to_all | solution.py:226

commit v2 on v1

v2 whole, which is shorter than its diff:
```python
import functools
import jax
import jax.numpy as jnp
from jax import lax
from jax.experimental import pallas as pl
from jax.experimental.pallas import tpu as pltpu
from jax.sharding import Mesh
from jax.sharding import PartitionSpec as P

F32, BF16, I32 = jnp.float32, jnp.bfloat16, jnp.int32
NT = (((1,), (1,)), ((), ()))
TN = (((0,), (0,)), ((), ()))


def iota(shape, dim):
    return lax.broadcasted_iota(I32, shape, dim)


def dot(a, b, dims=(((1,), (0,)), ((), ()))):
    return lax.dot_general(a, b, dims, preferred_element_type=F32)


def hot(mask):
    return jnp.where(mask, 1.0, 0.0).astype(BF16)


def spread_row():
    return hot(iota((32, 1024), 1) // 32 == iota((32, 1024), 0))


def spread_col():
    return hot(iota((32, 1024), 1) % 32 == iota((32, 1024), 0))


def fold_first(x):
    w = x[:, 0:128]
    for q in range(1, 8):
        w = w + x[:, q * 128 : (q + 1) * 128]
    return (w[:, 0:32] + w[:, 32:64]) + (w[:, 64:96] + w[:, 96:128])


def leaf_of(siz_ref, start, width):
    sizes = siz_ref[...].astype(F32)
    lower = iota((32, 32), 1) <= iota((32, 32), 0)
    ends = jnp.sum(jnp.where(lower, jnp.broadcast_to(sizes, (32, 32)), 0.0), axis=1, keepdims=True)
    pos = (iota((32, width), 1) + start).astype(F32)
    return jnp.sum(jnp.where(pos >= ends, 1.0, 0.0), axis=0, keepdims=True)


CH = 256


def up_kernel(vec, mor, siz, bas, lt, mt, rt, lc_out, root_out, term_out, masked, lt32):
    lt32[...] = lt[...].astype(F32)
    vx = jnp.concatenate([vec[:, h * 256 : (h + 1) * 256] for h in range(16)], axis=0).astype(BF16)

    def chunk(c, carry):
        at = pl.multiple_of(c * CH, CH)
        m = mor[:, pl.ds(at, CH)]
        lo, hi = m & 255, m >> 8
        pick = hot(iota((256, CH), 0) == lo)
        wide = dot(vx, pick)
        hib = jnp.broadcast_to(hi, (16, CH))
        sv = wide[0:16]
        for h in range(1, 16):
            sv = jnp.where(hib == h, wide[h * 16 : (h + 1) * 16], sv)
        leaf = jnp.broadcast_to(leaf_of(siz, at, CH), (16, CH)).astype(BF16)
        svb = sv.astype(BF16)
        for l in range(32):
            masked[l * 16 : (l + 1) * 16, pl.ds(at, CH)] = jnp.where(leaf == l, svb, jnp.zeros((), BF16))
        return carry

    lax.fori_loop(0, 4096 // CH, chunk, 0)
    lc = dot(masked[...], bas[...], NT).astype(BF16)
    lc_out[...] = lc
    erow = spread_row()
    root = jnp.zeros((16, 1024), F32)
    for m in range(4):
        acc = jnp.zeros((16, 1024), F32)
        x = dot(lc[m * 128 : (m + 1) * 128], erow)
        for l in range(8):
            acc = acc + x[l * 16 : (l + 1) * 16] * lt32[m * 8 + l : m * 8 + l + 1, :]
        mid = fold_first(acc).astype(BF16)
        root = root + dot(mid, erow) * mt[m : m + 1, :].astype(F32)
    root = fold_first(root).astype(BF16)
    root_out[...] = root
    term_out[...] = fold_first(dot(root, erow) * rt[...].astype(F32)).astype(BF16)


def pair_kernel(idx, lc, pairs, coup, far_out, s32, got, fwd, bwd):
    s32[...] = coup[...].astype(F32)
    erow, ecol = spread_row(), spread_col()
    back = hot(iota((1024, 32), 0) // 32 == iota((1024, 32), 1))

    def group(g, carry):
        for which, e in ((1, ecol), (0, erow)):
            for k in range(8):
                b = idx[which, g * 8 + k]
                got[k * 16 : (k + 1) * 16, :] = lc[pl.ds(pl.multiple_of(b * 16, 16), 16), :]
            x = dot(got[...], e)
            parts = [x[k * 16 : (k + 1) * 16] * s32[pl.ds(g * 8 + k, 1), :] for k in range(8)]
            if which == 1:
                y = dot(jnp.concatenate(parts, axis=0).astype(BF16), back)
                fwd[pl.ds(pl.multiple_of(g * 128, 128), 128), :] = y.astype(BF16)
            else:
                y = jnp.concatenate([fold_first(t) for t in parts], axis=0)
                bwd[pl.ds(pl.multiple_of(g * 128, 128), 128), :] = y.astype(BF16)
        return carry

    lax.fori_loop(0, 8, group, 0)
    wide = hot(iota((64, 1024), 1) // 16 == iota((64, 1024), 0))
    ids = dot(pairs[...].astype(F32).astype(BF16), wide)
    same = iota((512, 1024), 0) % 16 == iota((512, 1024), 1) % 16
    leaf = (iota((512, 1024), 0) // 16).astype(F32)
    far_out[...] = dot(hot(same & (leaf == ids[0:1])), fwd[...]) + dot(hot(same & (leaf == ids[1:2])), bwd[...])


def down_kernel(top, far, mor, siz, bas, lt, mt, out, scat):
    erow, ecol = spread_row(), spread_col()
    back = hot(iota((1024, 32), 0) // 32 == iota((1024, 32), 1))
    xt = dot(top[...], ecol)
    p = jnp.concatenate([xt * mt[m : m + 1, :].astype(F32) for m in range(4)], axis=0)
    ph = p.astype(BF16)
    pl_ = (p - ph.astype(F32)).astype(BF16)
    mid = (dot(ph, back) + dot(pl_, back)).astype(BF16)
    tots = []
    for m in range(4):
        x = dot(mid[m * 16 : (m + 1) * 16], ecol)
        q = jnp.concatenate(
            [x * lt[m * 8 + l : m * 8 + l + 1, :].astype(F32) for l in range(8)], axis=0
        ).astype(BF16)
        tots.append((dot(q, back) + far[m * 128 : (m + 1) * 128, :]).astype(BF16))
    tot = jnp.concatenate(tots, axis=0)

    def chunk(c, acc):
        at = pl.multiple_of(c * CH, CH)
        m = mor[:, pl.ds(at, CH)]
        lo, hi = m & 255, m >> 8
        pick = hot(iota((256, CH), 0) == lo)
        wide = dot(tot, bas[:, pl.ds(at, CH)])
        leaf = jnp.broadcast_to(leaf_of(siz, at, CH), (16, CH))
        o = wide[0:16]
        for l in range(1, 32):
            o = jnp.where(leaf == l, wide[l * 16 : (l + 1) * 16], o)
        ob = o.astype(BF16)
        hib = jnp.broadcast_to(hi, (16, CH)).astype(F32).astype(BF16)
        for h in range(16):
            scat[h * 16 : (h + 1) * 16, :] = jnp.where(hib == h, ob, jnp.zeros((), BF16))
        return acc + dot(scat[...], pick, NT)

    acc = lax.fori_loop(0, 4096 // CH, chunk, jnp.zeros((256, 256), F32))
    for h in range(16):
        out[:, h * 256 : (h + 1) * 256] = acc[h * 16 : (h + 1) * 16]


S = jax.ShapeDtypeStruct
VM = pltpu.VMEM


def up(vec, mor, siz, bas, lt, mt, rt):
    return pl.pallas_call(up_kernel, out_shape=(S((512, 32), BF16), S((16, 32), BF16), S((16, 32), BF16)),
        scratch_shapes=[VM((512, 4096), BF16), VM((32, 1024), F32)])(vec, mor, siz, bas, lt, mt, rt)


def pairs_(idx, lc, coup):
    vm = pl.BlockSpec(memory_space=pltpu.VMEM)
    return pl.pallas_call(pair_kernel, out_shape=S((512, 32), F32),
        in_specs=[pl.BlockSpec(memory_space=pltpu.SMEM), vm, vm, vm],
        scratch_shapes=[VM((64, 1024), F32), VM((128, 32), BF16), VM((1024, 32), BF16), VM((1024, 32), BF16)])(idx, lc, idx, coup)


def down(top, far, mor, siz, bas, lt, mt):
    return pl.pallas_call(down_kernel, out_shape=S((16, 4096), F32),
        scratch_shapes=[VM((256, CH), BF16)])(top, far, mor, siz, bas, lt, mt)


AXES = ("leaf_0", "leaf_1", "leaf_2", "leaf_3")
MESH = pl.DeviceIdType.MESH


def split2(x):
    hi = x.astype(BF16)
    return hi, (x - hi.astype(F32)).astype(BF16)


def pack_row(c):
    wide = dot(c, hot(iota((32, 128), 1) % 32 == iota((32, 128), 0)))
    wide = jnp.where(iota((16, 128), 1) // 32 == iota((16, 128), 0) % 4, wide, 0.0).astype(BF16)
    return dot(hot(iota((4, 16), 1) // 4 == iota((4, 16), 0)), wide)


def unpack_row(r):
    sel = hot(iota((16, 4), 0) // 4 == iota((16, 4), 1))
    hi, lo = split2(r)
    wide = dot(sel, hi) + dot(sel, lo)
    wide = jnp.where(iota((16, 128), 1) // 32 == iota((16, 128), 0) % 4, wide, 0.0)
    return (wide[:, 0:32] + wide[:, 32:64]) + (wide[:, 64:96] + wide[:, 96:128])


def sum_rows(ref, n):
    flat = ref[...].reshape(n * 4, 128)
    return dot(hot(iota((4, n * 4), 1) % 4 == iota((4, n * 4), 0)), flat)


def back_weights(c, w):
    cex = dot(c, hot(iota((16, 512), 1) // 32 == iota((16, 512), 0)), TN)
    same = iota((32, 512), 1) % 32 == iota((32, 512), 0)
    for i in range(32):
        row = jnp.broadcast_to(cex[i : i + 1, :], (32, 512))
        w[i * 32 : (i + 1) * 32, :] = jnp.where(same, row, 0.0).astype(BF16)


def forward_sum(blocks, chosen):
    same = iota((32, 512), 1) % 32 == iota((32, 512), 0)
    rows = []
    for q in range(4):
        part = dot(blocks[:, q * 256 : (q + 1) * 256], chosen, TN)
        for i in range(8):
            rows.append(jnp.sum(jnp.where(same, part[i * 32 : (i + 1) * 32], 0.0), axis=0, keepdims=True))
    y = jnp.concatenate(rows, axis=0)
    hi, lo = split2(y)
    sel = hot(iota((16, 512), 1) // 32 == iota((16, 512), 0))
    return dot(sel, hi, NT) + dot(sel, lo, NT)


def lanes_of(ref, n):
    return jnp.concatenate([ref[:, q, :] for q in range(4)], axis=1)


def comm_kernel(dims, root_ref, term_ref, partner, dcoup, gpart, gcoup, rt, top_out,
                ca, rsb, rx, sb, rr, gx, sgx, pgx, gcb, tb, gr, w, rowb, termb, pgs, gcrow,
                send, recv):
    nx, ny, nz = dims
    chips = nx * ny * nz
    groups = chips // 4
    x, y, z, c = [lax.axis_index(a) for a in AXES]
    chip = (x * ny + y) * nz + z
    g = chip // 4
    zq = z % 4
    k = zq * 2 + c

    def at_chip(d):
        dx = d // (ny * nz) + nx // 2
        dy = (d // nz) % ny + ny // 2
        dz = d % nz + nz // 2
        return (x + dx) % nx, (y + dy) % ny, (z + dz) % nz

    own = ((nx - nx // 2) % nx * ny + (ny - ny // 2) % ny) * nz + (nz - nz // 2) % nz

    def every_chip(f):
        lax.fori_loop(0, own, lambda d, s: (f(*at_chip(d)), s)[1], 0)
        lax.fori_loop(own + 1, chips, lambda d, s: (f(*at_chip(d)), s)[1], 0)

    def mate(j):
        r = (k + j) % 8
        return (x, y, z - zq + r // 2, r % 2)

    halves = nz // 4

    def group_peer(d):
        h = (g + d) % groups
        return h, (h // (ny * halves), (h // halves) % ny, (h % halves) * 4 + zq, c)

    def every_group(f):
        lax.fori_loop(1, groups, lambda d, s: (f(*group_peer(d)), s)[1], 0)

    sibling = (x, y, z, 1 - c)

    def push(src, dst, i, to):
        pltpu.make_async_remote_copy(src, dst, send.at[i], recv.at[i], device_id=to, device_id_type=MESH).start()

    def await_(src, dst, i, to, which):
        cp = pltpu.make_async_remote_copy(src, dst, send.at[i], recv.at[i], device_id=to, device_id_type=MESH)
        (cp.wait_recv if which else cp.wait_send)()

    def got(ref, i):
        await_(ref, ref, i, sibling, True)

    def sent(ref, i):
        await_(ref, ref, i, sibling, False)

    bar = pltpu.get_barrier_semaphore()

    def greet(to):
        pl.semaphore_signal(bar, inc=1, device_id=to, device_id_type=MESH)

    every_chip(lambda a, b, d: greet((a, b, d, c)))
    others = 0
    for j in range(1, 8):
        r = (k + j) % 8

        @pl.when(r % 2 != c)
        def _():
            greet(mate(j))

    pgs[...] = jnp.zeros((1, 128), I32)
    pgs[:, 0:4] = gpart[...]
    rowb[...] = pack_row(root_ref[...]).astype(BF16)
    termb[...] = pack_row(term_ref[...]).astype(BF16)
    pl.semaphore_wait(bar, chips - 1 + 4)

    for j in range(1, 8):
        push(termb, gx.at[k], 0, mate(j))
    for j in range(1, 8):
        push(gcoup, sgx.at[k], 1, mate(j))
        push(pgs, pgx.at[k], 2, mate(j))
    every_chip(lambda a, b, d: push(rowb, ca.at[c, chip], 3, (a, b, d, c)))
    gx[k] = termb[...]
    sgx[k] = gcoup[...]
    pgx[k] = pgs[...]
    ca[c, chip] = rowb[...]

    back_weights(root_ref[...], w)
    bk = dot(dcoup[...], w[...]).astype(BF16)
    for half in range(2):
        ids = iota((chips, 128), 0) * 2 + half
        hotb = hot(ids == jnp.broadcast_to(partner[...], (chips, 128)))
        r = dot(hotb, bk).astype(BF16)
        for q in range(4):
            rsb[half, :, q, :] = r[:, q * 128 : (q + 1) * 128]
    push(rsb.at[1 - c], rx, 4, sibling)

    got(gx.at[pl.ds(0, 7)], 0)
    gcoef = sum_rows(gx, 8).astype(BF16)
    gcrow[...] = gcoef
    every_group(lambda h, to: push(gcrow, gcb.at[g], 5, to))
    gcb[g] = gcoef

    got(rx, 4)
    sb[...] = (rsb[c].astype(F32) + rx[...].astype(F32)).astype(BF16)

    def send_back(a, b, d):
        push(sb.at[(a * ny + b) * nz + d], rr.at[chip], 6, (a, b, d, c))

    every_chip(send_back)
    rr[chip] = sb[chip]

    got(sgx.at[pl.ds(0, 7)], 1)
    got(pgx.at[pl.ds(0, 7)], 2)
    sg = sgx[...].reshape(32, 1024)
    p8 = pgx[...].reshape(8, 128).astype(F32).astype(BF16)[:, 0:4]
    spread = dot(p8, hot(iota((4, 32), 1) % 4 == iota((4, 32), 0)))
    pair = jnp.sum(jnp.where(iota((8, 32), 1) // 4 == iota((8, 32), 0), spread, 0.0), axis=0, keepdims=True)
    hotg = hot(iota((groups, 32), 0).astype(F32) == jnp.broadcast_to(pair, (groups, 32)))
    back_weights(unpack_row(gcoef.astype(F32)).astype(BF16), w)
    t = dot(hotg, dot(sg, w[...]).astype(BF16)).astype(BF16)
    for q in range(4):
        tb[:, q, :] = t[:, q * 128 : (q + 1) * 128]
    every_group(lambda h, to: push(tb.at[h], gr.at[g], 7, to))
    gr[g] = tb[g]

    got(ca.at[0, pl.ds(0, chips - 1)], 3)
    push(ca.at[c], ca.at[c], 8, sibling)
    got(ca.at[0], 8)
    near = jnp.zeros((128, 512), F32)
    for half in range(2):
        ids = iota((chips, 128), 0) * 2 + half
        hotb = hot(ids == jnp.broadcast_to(partner[...], (chips, 128)))
        near = near + dot(hotb, lanes_of(ca.at[half], chips), TN)
    root_far = forward_sum(dcoup[...], near.astype(BF16))
    got(gcb.at[pl.ds(0, groups - 1)], 5)
    far = dot(hotg, lanes_of(gcb, groups), TN).astype(BF16)
    group_far = forward_sum(sg, far)

    got(rr.at[pl.ds(0, chips - 1)], 6)
    root_far = root_far + unpack_row(sum_rows(rr, chips))
    got(gr.at[pl.ds(0, groups - 1)], 7)
    group_far = (group_far + unpack_row(sum_rows(gr, groups))).astype(BF16)
    ecol = spread_col()
    back = hot(iota((1024, 32), 0) // 32 == iota((1024, 32), 1))
    hi, lo = split2(dot(group_far, ecol) * rt[...].astype(F32))
    top_out[...] = (root_far + dot(hi, back) + dot(lo, back)).astype(BF16)

    sent(gx.at[pl.ds(0, 7)], 0)
    sent(sgx.at[pl.ds(0, 7)], 1)
    sent(pgx.at[pl.ds(0, 7)], 2)
    sent(ca.at[0, pl.ds(0, chips - 1)], 3)
    sent(rx, 4)
    sent(gcb.at[pl.ds(0, groups - 1)], 5)
    sent(rr.at[pl.ds(0, chips - 1)], 6)
    sent(gr.at[pl.ds(0, groups - 1)], 7)
    sent(ca.at[0], 8)


def comm_scratch(chips):
    groups = chips // 4
    b = lambda *s: pltpu.VMEM(s, BF16)
    return [b(2, chips, 4, 128), b(2, chips, 4, 128), b(chips, 4, 128), b(chips, 4, 128), b(chips, 4, 128),
            b(8, 4, 128), b(8, 4, 1024), pltpu.VMEM((8, 1, 128), I32), b(groups, 4, 128), b(groups, 4, 128),
            b(groups, 4, 128), b(1024, 512), b(4, 128), b(4, 128), pltpu.VMEM((1, 128), I32), b(4, 128),
            pltpu.SemaphoreType.DMA((9,)), pltpu.SemaphoreType.DMA((9,))]


def comm(dims, root, term, partner, dcoup, gpart, gcoup, rt):
    chips = dims[0] * dims[1] * dims[2]
    return pl.pallas_call(functools.partial(comm_kernel, dims), out_shape=jax.ShapeDtypeStruct((16, 32), BF16),
        scratch_shapes=comm_scratch(chips),
        compiler_params=pltpu.CompilerParams(collective_id=0, has_side_effects=True))(
            root, term, partner, dcoup, gpart, gcoup, rt)


def body(dims, vec, mor, siz, bas, lt, mt, rt, pairs, lcoup, partner, dcoup, gpart, gcoup):
    lc, root, term = up(vec, mor, siz, bas, lt, mt, rt)
    top = comm(dims, root, term, partner, dcoup, gpart, gcoup, rt)
    far = pairs_(pairs, lc, lcoup)
    return down(top, far, mor, siz, bas, lt, mt)


def solution(mesh):
    split = Mesh(mesh.devices.reshape(4, 8, 8, 2), AXES)
    rows, cols = P(AXES, None), P(None, AXES)
    in_specs = (cols, rows, rows, cols, rows, rows, rows, cols, rows, rows, rows, rows, rows)
    step = functools.partial(body, (4, 8, 8))
    return jax.shard_map(step, mesh=split, in_specs=in_specs, out_specs=cols, check_vma=False)
```

time: 156 us -> 82.4 us (0.53)
  blocking collectives: 76.8 us -> 0 us
  Pallas kernels: 26.6 us -> 82.2 us
  waiting for transfers between devices: 26.5 us -> 0 us
  starting transfers between devices: 14.5 us -> 0 us
  local copies, waits for them, and re-layouts: 6.92 us -> 0 us
  matrix products: 3.14 us -> 0 us
    all_to_all x2 -> x0, blocking collectives: 76.8 us -> none  [the longest x1 57.8 us: sum_at_owner(): parts = lax.all_to_all(split_up(array, dim, peers), axis, 0, 0, tiled=True)]
    pallas_call x0 -> x1, Pallas kernels: none -> 55.6 us  [comm(): pl.pallas_call(functools.partial(comm_kernel, dims), out_shape=jax.ShapeD...]
    all_to_all x2 -> x0, waiting for transfers between devices: 26.5 us -> none  [the longest x1 24 us: from_everyone(): lax.all_to_all(jnp.broadcast_to(array[None], (peers, *array.shape)), axis...]
    all_to_all x2 -> x0, starting transfers between devices: 14.5 us -> none  [the longest x1 9.67 us: from_everyone(): lax.all_to_all(jnp.broadcast_to(array[None], (peers, *array.shape)), axis...]
    dot_general x10 -> x0, matrix products: 3.14 us -> none  [the longest x1 0.77 us: body(): jnp.dot(root_map, group_far, preferred_element_type=jnp.float32)]
    transpose x3 -> x0, local copies, waits for them, and re-layouts: 2.74 us -> none  [the longest x1 1.22 us: split_up(): return jnp.moveaxis(parts, dim, 0)]
    broadcast_in_dim x4 -> x0, local copies, waits for them, and re-layouts: 1.86 us -> none  [the longest x3 1.75 us: from_everyone(): jnp.broadcast_to(array[None], (peers, *array.shape))]
  transfers between devices with their start and end apart: 2 -> 0, of which waited for: 2 -> 0; matrix products, arithmetic and copies ran while one was open for 1% -> 0% of each run, Pallas kernels for 5% -> 0%
where the time goes in v2:
time: 82.4 us; the launch traced here: 82.2 us
  Pallas kernels  82.2 us (100%)
    pallas_call x1, Pallas kernels, comm(): pl.pallas_call(functools.partial(comm_kernel, dims), out_shape=jax.ShapeD...  55.6 us
    pallas_call x1, Pallas kernels, down(): pl.pallas_call(down_kernel, out_shape=S((16, 4096), F32), scratch_shapes=...  10.3 us
    pallas_call x1, Pallas kernels, up(): pl.pallas_call(up_kernel, out_shape=(S((512, 32), BF16), S((16, 32), BF16...  9.12 us
    pallas_call x1, Pallas kernels, pairs_(): pl.pallas_call(pair_kernel, out_shape=S((512, 32), F32), in_specs=[pl.Blo...  7.08 us

profile of v2, /device:TPU:1, one launch (start us, length us, event | category | flops | bytes accessed | tf_op | source)
XLA Modules:
  0.0 82.2 jit_solution(12412763786607372524)
XLA Ops:
  0.0 9.1 %shard_map.127 = (bf16[512,32]{1,0:T(8,128)(2,1)}, bf16[16,32]{1,0:T(8,128)(2,1)}, bf16[16,32]{1,0:T(8,128)(2,1)}) custom-call(f32[16,4096]{1,0:T(8,128)} %vec.1, s32[1,4096]{1,0:T(1,128)} %mor.3, s32[1,32]{1,0:T(1,128)} %siz.3, bf16[32,4096]{1,0:T(8,128)(2,1)} %bas.3, bf16[32,1024]{1,0:T(8,128)(2,1)} %lt.3, bf16[4,1024]{1,0:T(4,128)(2,1)} %mt.3, ...), custom_call_target="tpu_custom_call" | custom-call | tf_op jit(solution)/shard_map/pallas_call | solution.py:161
  9.1 55.6 %shard_map.128.top = bf16[16,32]{1,0:T(8,128)(2,1)} custom-call(bf16[16,32]{1,0:T(8,128)(2,1)} %get-tuple-element.8.root_ref, bf16[16,32]{1,0:T(8,128)(2,1)} %get-tuple-element.9.term_ref, s32[1,128]{1,0:T(1,128)} %partner.1, bf16[128,1024]{1,0:T(8,128)(2,1)} %dcoup.1, s32[1,4]{1,0:T(1,128)} %gpart.1, bf16[4,1024]{1,0:T(4,128)(2,1)} %gcoup.1, bf16[1,1024]{1,0:T(2,128)(2,1)} %rt.3), custom_call_target="tpu_custom_call" | custom-call | tf_op jit(solution)/shard_map/pallas_call | solution.py:396
  64.8 7.1 %shard_map.129.far = f32[512,32]{1,0:T(8,128)} custom-call(s32[2,64]{1,0:T(2,128)} %pairs.1, bf16[512,32]{1,0:T(8,128)(2,1)} %get-tuple-element.10.lc, s32[2,64]{1,0:T(2,128)} %pairs.1, bf16[64,1024]{1,0:T(8,128)(2,1)} %coup.1), custom_call_target="tpu_custom_call" | custom-call | tf_op jit(solution)/shard_map/pallas_call | solution.py:167
  71.8 10.3 %shard_map.130 = f32[16,4096]{1,0:T(8,128)} custom-call(bf16[16,32]{1,0:T(8,128)(2,1)} %shard_map.128.top, f32[512,32]{1,0:T(8,128)} %shard_map.129.far, s32[1,4096]{1,0:T(1,128)} %mor.3, s32[1,32]{1,0:T(1,128)} %siz.3, bf16[32,4096]{1,0:T(8,128)(2,1)} %bas.3, bf16[32,1024]{1,0:T(8,128)(2,1)} %lt.3, bf16[4,1024]{1,0:T(4,128)(2,1)} %mt.3), custom_call_target="tpu_custom_call" | custom-call | tf_op jit(solution)/shard_map/pallas_call | solution.py:173

commit v3 on v2

v3 whole, which is shorter than its diff:
```python
import functools
import jax
import jax.numpy as jnp
from jax import lax
from jax.experimental import pallas as pl
from jax.experimental.pallas import tpu as pltpu
from jax.sharding import Mesh
from jax.sharding import PartitionSpec as P

F32, BF16, I32 = jnp.float32, jnp.bfloat16, jnp.int32
NT = (((1,), (1,)), ((), ()))
TN = (((0,), (0,)), ((), ()))


def iota(shape, dim):
    return lax.broadcasted_iota(I32, shape, dim)


def dot(a, b, dims=(((1,), (0,)), ((), ()))):
    return lax.dot_general(a, b, dims, preferred_element_type=F32)


def hot(mask):
    return jnp.where(mask, 1.0, 0.0).astype(BF16)


def spread_row():
    return hot(iota((32, 1024), 1) // 32 == iota((32, 1024), 0))


def spread_col():
    return hot(iota((32, 1024), 1) % 32 == iota((32, 1024), 0))


def fold_first(x):
    w = x[:, 0:128]
    for q in range(1, 8):
        w = w + x[:, q * 128 : (q + 1) * 128]
    return (w[:, 0:32] + w[:, 32:64]) + (w[:, 64:96] + w[:, 96:128])


def leaf_of(siz_ref, start, width):
    sizes = siz_ref[...].astype(F32)
    lower = iota((32, 32), 1) <= iota((32, 32), 0)
    ends = jnp.sum(jnp.where(lower, jnp.broadcast_to(sizes, (32, 32)), 0.0), axis=1, keepdims=True)
    pos = (iota((32, width), 1) + start).astype(F32)
    return jnp.sum(jnp.where(pos >= ends, 1.0, 0.0), axis=0, keepdims=True)


CH = 256


def down_kernel(top, far, mor, siz, bas, lt, mt, out, scat):
    erow, ecol = spread_row(), spread_col()
    back = hot(iota((1024, 32), 0) // 32 == iota((1024, 32), 1))
    xt = dot(top[...], ecol)
    p = jnp.concatenate([xt * mt[m : m + 1, :].astype(F32) for m in range(4)], axis=0)
    ph = p.astype(BF16)
    pl_ = (p - ph.astype(F32)).astype(BF16)
    mid = (dot(ph, back) + dot(pl_, back)).astype(BF16)
    tots = []
    for m in range(4):
        x = dot(mid[m * 16 : (m + 1) * 16], ecol)
        q = jnp.concatenate(
            [x * lt[m * 8 + l : m * 8 + l + 1, :].astype(F32) for l in range(8)], axis=0
        ).astype(BF16)
        tots.append((dot(q, back) + far[m * 128 : (m + 1) * 128, :]).astype(BF16))
    tot = jnp.concatenate(tots, axis=0)

    def chunk(c, acc):
        at = pl.multiple_of(c * CH, CH)
        m = mor[:, pl.ds(at, CH)]
        lo, hi = m & 255, m >> 8
        pick = hot(iota((256, CH), 0) == lo)
        wide = dot(tot, bas[:, pl.ds(at, CH)])
        leaf = jnp.broadcast_to(leaf_of(siz, at, CH), (16, CH))
        o = wide[0:16]
        for l in range(1, 32):
            o = jnp.where(leaf == l, wide[l * 16 : (l + 1) * 16], o)
        ob = o.astype(BF16)
        hib = jnp.broadcast_to(hi, (16, CH)).astype(F32).astype(BF16)
        for h in range(16):
            scat[h * 16 : (h + 1) * 16, :] = jnp.where(hib == h, ob, jnp.zeros((), BF16))
        return acc + dot(scat[...], pick, NT)

    acc = lax.fori_loop(0, 4096 // CH, chunk, jnp.zeros((256, 256), F32))
    for h in range(16):
        out[:, h * 256 : (h + 1) * 256] = acc[h * 16 : (h + 1) * 16]


S = jax.ShapeDtypeStruct
VM = pltpu.VMEM


def down(top, far, mor, siz, bas, lt, mt):
    return pl.pallas_call(down_kernel, out_shape=S((16, 4096), F32),
        scratch_shapes=[VM((256, CH), BF16)])(top, far, mor, siz, bas, lt, mt)


AXES = ("leaf_0", "leaf_1", "leaf_2", "leaf_3")
MESH = pl.DeviceIdType.MESH


def split2(x):
    hi = x.astype(BF16)
    return hi, (x - hi.astype(F32)).astype(BF16)


def pack_row(c):
    wide = dot(c, hot(iota((32, 128), 1) % 32 == iota((32, 128), 0)))
    wide = jnp.where(iota((16, 128), 1) // 32 == iota((16, 128), 0) % 4, wide, 0.0).astype(BF16)
    return dot(hot(iota((4, 16), 1) // 4 == iota((4, 16), 0)), wide)


def unpack_row(r):
    sel = hot(iota((16, 4), 0) // 4 == iota((16, 4), 1))
    hi, lo = split2(r)
    wide = dot(sel, hi) + dot(sel, lo)
    wide = jnp.where(iota((16, 128), 1) // 32 == iota((16, 128), 0) % 4, wide, 0.0)
    return (wide[:, 0:32] + wide[:, 32:64]) + (wide[:, 64:96] + wide[:, 96:128])


def sum_rows(ref, n):
    flat = ref[...].reshape(n * 4, 128)
    return dot(hot(iota((4, n * 4), 1) % 4 == iota((4, n * 4), 0)), flat)


def back_weights(c, w):
    cex = dot(c, hot(iota((16, 512), 1) // 32 == iota((16, 512), 0)), TN)
    same = iota((32, 512), 1) % 32 == iota((32, 512), 0)
    for i in range(32):
        row = jnp.broadcast_to(cex[i : i + 1, :], (32, 512))
        w[i * 32 : (i + 1) * 32, :] = jnp.where(same, row, 0.0).astype(BF16)


def forward_sum(blocks, chosen):
    same = iota((32, 512), 1) % 32 == iota((32, 512), 0)
    rows = []
    for q in range(4):
        part = dot(blocks[:, q * 256 : (q + 1) * 256], chosen, TN)
        for i in range(8):
            rows.append(jnp.sum(jnp.where(same, part[i * 32 : (i + 1) * 32], 0.0), axis=0, keepdims=True))
    y = jnp.concatenate(rows, axis=0)
    hi, lo = split2(y)
    sel = hot(iota((16, 512), 1) // 32 == iota((16, 512), 0))
    return dot(sel, hi, NT) + dot(sel, lo, NT)


def lanes_of(x):
    return x.reshape(x.shape[0], 512)


def add_all(terms):
    return functools.reduce(lambda a, b: a + b, [t.astype(F32) for t in terms]).astype(BF16)


def mega_kernel(dims, vec, mor, siz, bas, lt, mt, rt, pairs, lcoup, partner, dcoup, gpart, gcoup,
                top_out, far_out,
                masked, lt32, lc, s32, idcol, fwd, bwd,
                ca, rsb, rx, sb, rx2, sb2, rr, gx, sgx, pgx, gcb, tb, gr2, tb2, gr, w,
                rowb, termb, pgs, gcrow, send, recv):
    nx, ny, nz = dims
    halves = nz // 4
    plane, pgs_n = ny * nz, ny * halves
    x, y, z, c = [lax.axis_index(a) for a in AXES]
    zq, zh = z % 4, z // 4
    k = zq * 2 + c
    yz = y * nz + z
    pg = y * halves + zh
    xs = [(x + j) % nx for j in range(nx)]
    ys = [(y + j) % ny for j in range(ny)]
    zs = [(z + j) % nz for j in range(nz)]
    gz = [((zh + j) % halves) * 4 + zq for j in range(halves)]
    far_first = lambda o: -(min(o[0], ny - o[0]) + min(o[1], nz - o[1]))
    offs = sorted([(a, b) for a in range(ny) for b in range(nz) if a or b], key=far_first)
    goffs = sorted([(a, b) for a in range(ny) for b in range(halves) if a or b], key=lambda o: -min(o[0], ny - o[0]))
    sibling = (x, y, z, 1 - c)

    def mate(j):
        r = (k + j) % 8
        return (x, y, zh * 4 + r // 2, r % 2)

    def push(src, dst, i, to):
        pltpu.make_async_remote_copy(src, dst, send.at[i], recv.at[i], device_id=to, device_id_type=MESH).start()

    def settle(ref, i, which):
        cp = pltpu.make_async_remote_copy(
            ref, ref, send.at[i], recv.at[i], device_id=sibling, device_id_type=MESH
        )
        (cp.wait_recv if which else cp.wait_send)()

    def got(ref, i):
        settle(ref, i, True)

    def sent(ref, i):
        settle(ref, i, False)

    bar = pltpu.get_barrier_semaphore()

    def greet(to):
        pl.semaphore_signal(bar, inc=1, device_id=to, device_id_type=MESH)

    for a, b in offs:
        greet((x, ys[a], zs[b], c))
    for j in range(1, nx):
        greet((xs[j], y, z, c))
    for j in range(1, 8):

        @pl.when((k + j) % 2 != c)
        def _():
            greet(mate(j))

    pgs[...] = jnp.zeros((1, 128), I32)
    pgs[:, 0:4] = gpart[...]
    lt32[...] = lt[...].astype(F32)
    vx = jnp.concatenate([vec[:, h * 256 : (h + 1) * 256] for h in range(16)], axis=0).astype(BF16)

    def chunk(i, carry):
        at = pl.multiple_of(i * CH, CH)
        m = mor[:, pl.ds(at, CH)]
        lo, hi = m & 255, m >> 8
        wide = dot(vx, hot(iota((256, CH), 0) == lo))
        hib = jnp.broadcast_to(hi, (16, CH))
        sv = wide[0:16]
        for h in range(1, 16):
            sv = jnp.where(hib == h, wide[h * 16 : (h + 1) * 16], sv)
        leaf = jnp.broadcast_to(leaf_of(siz, at, CH), (16, CH)).astype(BF16)
        svb = sv.astype(BF16)
        for l in range(32):
            masked[l * 16 : (l + 1) * 16, pl.ds(at, CH)] = jnp.where(leaf == l, svb, jnp.zeros((), BF16))
        return carry

    lax.fori_loop(0, 4096 // CH, chunk, 0)
    lcv = dot(masked[...], bas[...], NT).astype(BF16)
    lc[...] = lcv
    erow, ecol = spread_row(), spread_col()
    root = jnp.zeros((16, 1024), F32)
    for m in range(4):
        acc = jnp.zeros((16, 1024), F32)
        wide = dot(lcv[m * 128 : (m + 1) * 128], erow)
        for l in range(8):
            acc = acc + wide[l * 16 : (l + 1) * 16] * lt32[m * 8 + l : m * 8 + l + 1, :]
        mid = fold_first(acc).astype(BF16)
        root = root + dot(mid, erow) * mt[m : m + 1, :].astype(F32)
    root = fold_first(root).astype(BF16)
    term = fold_first(dot(root, erow) * rt[...].astype(F32)).astype(BF16)
    termb[...] = pack_row(term).astype(BF16)
    rowb[...] = pack_row(root).astype(BF16)
    pl.semaphore_wait(bar, plane - 1 + nx - 1 + 4)

    for j in range(1, 8):
        push(termb, gx.at[k], 0, mate(j))
    for a, b in offs:
        push(rowb, ca.at[c, x, yz], 3, (x, ys[a], zs[b], c))
    for j in range(1, 8):
        push(gcoup, sgx.at[k], 1, mate(j))
        push(pgs, pgx.at[k], 2, mate(j))
    gx[k] = termb[...]
    sgx[k] = gcoup[...]
    pgx[k] = pgs[...]
    ca[c, x, yz] = rowb[...]

    back_weights(root, w)
    bk = dot(dcoup[...], w[...]).astype(BF16)
    chips = nx * plane
    for half in range(2):
        ids = iota((chips, 128), 0) * 2 + half
        hotb = hot(ids == jnp.broadcast_to(partner[...], (chips, 128)))
        rsb[half] = dot(hotb, bk).astype(BF16).reshape(nx, plane, 4, 128)
    push(rsb.at[1 - c], rx, 4, sibling)

    got(gx.at[pl.ds(0, 7)], 0)
    gcoef = sum_rows(gx, 8).astype(BF16)
    gcrow[...] = gcoef
    for a, b in goffs:
        push(gcrow, gcb.at[x, pg], 5, (x, ys[a], gz[b], c))
    gcb[x, pg] = gcoef

    got(sgx.at[pl.ds(0, 7)], 1)
    got(pgx.at[pl.ds(0, 7)], 2)
    sg = sgx[...].reshape(32, 1024)
    groups = nx * pgs_n
    p8 = pgx[...].reshape(8, 128).astype(F32).astype(BF16)[:, 0:4]
    spread = dot(p8, hot(iota((4, 32), 1) % 4 == iota((4, 32), 0)))
    gpair = jnp.sum(jnp.where(iota((8, 32), 1) // 4 == iota((8, 32), 0), spread, 0.0), axis=0, keepdims=True)
    hotg = hot(iota((groups, 32), 0).astype(F32) == jnp.broadcast_to(gpair, (groups, 32)))
    back_weights(unpack_row(gcoef.astype(F32)).astype(BF16), w)
    tb[...] = dot(hotg, dot(sg, w[...]).astype(BF16)).astype(BF16).reshape(nx, pgs_n, 4, 128)
    for j in range(1, nx):
        push(tb.at[xs[j]], gr2.at[j - 1], 7, (xs[j], y, z, c))

    got(rx, 4)
    sb[...] = add_all([rsb[c], rx[...]])
    for j in range(1, nx):
        push(sb.at[xs[j]], rx2.at[j - 1], 6, (xs[j], y, z, c))

    s32[...] = lcoup[...].astype(F32)
    each = hot(iota((64, 1024), 1) // 16 == iota((64, 1024), 0))
    pairsb = pairs[...].astype(F32).astype(BF16)
    idcol[...] = dot(each, pairsb, (((0,), (1,)), ((), ())))
    back = hot(iota((1024, 32), 0) // 32 == iota((1024, 32), 1))

    def leaf_group(gi, carry):
        at = pl.multiple_of(gi * 128, 128)
        eye = iota((128, 512), 0) % 16 == iota((128, 512), 1) % 16
        for which, e in ((1, ecol), (0, erow)):
            leaf = jnp.broadcast_to(idcol[pl.ds(at, 128), which : which + 1], (128, 512))
            chosen = dot(hot(eye & (leaf == (iota((128, 512), 1) // 16).astype(F32))), lc[...]).astype(BF16)
            wide = dot(chosen, e)
            parts = [wide[t * 16 : (t + 1) * 16] * s32[pl.ds(gi * 8 + t, 1), :] for t in range(8)]
            if which == 1:
                out = dot(jnp.concatenate(parts, axis=0).astype(BF16), back)
                fwd[pl.ds(at, 128), :] = out.astype(BF16)
            else:
                out = jnp.concatenate([fold_first(t) for t in parts], axis=0)
                bwd[pl.ds(at, 128), :] = out.astype(BF16)
        return carry

    lax.fori_loop(0, 3, leaf_group, 0)

    got(ca.at[c, x, pl.ds(0, plane - 1)], 3)
    for j in range(1, nx):
        push(ca.at[c, x], ca.at[c, x], 9, (xs[j], y, z, c))
    push(ca.at[c, x], ca.at[c, x], 8, sibling)

    got(rx2, 6)
    sb2[...] = add_all([sb[x]] + [rx2[j] for j in range(nx - 1)])
    for a, b in offs:
        push(sb2.at[ys[a] * nz + zs[b]], rr.at[yz], 10, (x, ys[a], zs[b], c))
    rr[yz] = sb2[yz]
    got(gr2, 7)
    tb2[...] = add_all([tb[x]] + [gr2[j] for j in range(nx - 1)])
    for a, b in goffs:
        push(tb2.at[ys[a] * halves + (zh + b) % halves], gr.at[pg], 11, (x, ys[a], gz[b], c))
    gr[pg] = tb2[pg]

    got(gcb.at[x, pl.ds(0, pgs_n - 1)], 5)
    for j in range(1, nx):
        push(gcb.at[x], gcb.at[x], 12, (xs[j], y, z, c))

    lax.fori_loop(3, 8, leaf_group, 0)

    got(ca.at[c, pl.ds(0, nx - 1)], 9)
    for j in range(1, nx):
        push(ca.at[c, xs[j]], ca.at[c, xs[j]], 13, sibling)
    ids = dot(pairsb, each)
    same = iota((512, 1024), 0) % 16 == iota((512, 1024), 1) % 16
    leaf = (iota((512, 1024), 0) // 16).astype(F32)
    far_out[...] = dot(hot(same & (leaf == ids[0:1])), fwd[...]) + dot(hot(same & (leaf == ids[1:2])), bwd[...])
    got(ca.at[c, x], 8)
    got(ca.at[c, pl.ds(0, nx - 1)], 13)
    near = jnp.zeros((128, 512), F32)
    for half in range(2):
        ids = iota((chips, 128), 0) * 2 + half
        hotb = hot(ids == jnp.broadcast_to(partner[...], (chips, 128)))
        near = near + dot(hotb, lanes_of(ca[half].reshape(chips, 4, 128)), TN)
    root_far = forward_sum(dcoup[...], near.astype(BF16))
    got(gcb.at[pl.ds(0, nx - 1)], 12)
    far = dot(hotg, lanes_of(gcb[...].reshape(groups, 4, 128)), TN).astype(BF16)
    group_far = forward_sum(sg, far)

    got(rr.at[pl.ds(0, plane - 1)], 10)
    root_far = root_far + unpack_row(sum_rows(rr, plane))
    got(gr.at[pl.ds(0, pgs_n - 1)], 11)
    group_far = (group_far + unpack_row(sum_rows(gr, pgs_n))).astype(BF16)
    hi, lo = split2(dot(group_far, ecol) * rt[...].astype(F32))
    top_out[...] = (root_far + dot(hi, back) + dot(lo, back)).astype(BF16)

    sent(gx.at[pl.ds(0, 7)], 0)
    sent(sgx.at[pl.ds(0, 7)], 1)
    sent(pgx.at[pl.ds(0, 7)], 2)
    sent(ca.at[c, x, pl.ds(0, plane - 1)], 3)
    sent(rx, 4)
    sent(gcb.at[x, pl.ds(0, pgs_n - 1)], 5)
    sent(rx2, 6)
    sent(gr2, 7)
    sent(ca.at[c, x], 8)
    sent(ca.at[c, pl.ds(0, nx - 1)], 9)
    sent(rr.at[pl.ds(0, plane - 1)], 10)
    sent(gr.at[pl.ds(0, pgs_n - 1)], 11)
    sent(gcb.at[pl.ds(0, nx - 1)], 12)
    sent(ca.at[c, pl.ds(0, nx - 1)], 13)


def mega(dims, vec, mor, siz, bas, lt, mt, rt, pairs, lcoup, partner, dcoup, gpart, gcoup):
    nx, ny, nz = dims
    plane, pgn = ny * nz, ny * nz // 4
    b = lambda *s: pltpu.VMEM(s, BF16)
    vm = pl.BlockSpec(memory_space=pltpu.VMEM)
    scratch = [
        b(512, 4096), VM((32, 1024), F32), b(512, 32), VM((64, 1024), F32), VM((1024, 2), F32), b(1024, 32), b(1024, 32),
        b(2, nx, plane, 4, 128), b(2, nx, plane, 4, 128), b(nx, plane, 4, 128), b(nx, plane, 4, 128),
        b(nx - 1, plane, 4, 128), b(plane, 4, 128), b(plane, 4, 128),
        b(8, 4, 128), b(8, 4, 1024), VM((8, 1, 128), I32),
        b(nx, pgn, 4, 128), b(nx, pgn, 4, 128), b(nx - 1, pgn, 4, 128), b(pgn, 4, 128), b(pgn, 4, 128),
        b(1024, 512), b(4, 128), b(4, 128), VM((1, 128), I32), b(4, 128),
        pltpu.SemaphoreType.DMA((14,)), pltpu.SemaphoreType.DMA((14,)),
    ]
    return pl.pallas_call(
        functools.partial(mega_kernel, dims),
        out_shape=(S((16, 32), BF16), S((512, 32), F32)),
        in_specs=[vm] * 13,
        scratch_shapes=scratch,
        compiler_params=pltpu.CompilerParams(collective_id=0, has_side_effects=True),
    )(vec, mor, siz, bas, lt, mt, rt, pairs, lcoup, partner, dcoup, gpart, gcoup)


def body(dims, vec, mor, siz, bas, lt, mt, rt, pairs, lcoup, partner, dcoup, gpart, gcoup):
    top, far = mega(dims, vec, mor, siz, bas, lt, mt, rt, pairs, lcoup, partner, dcoup, gpart, gcoup)
    return down(top, far, mor, siz, bas, lt, mt)


def solution(mesh):
    split = Mesh(mesh.devices.reshape(4, 8, 8, 2), AXES)
    rows, cols = P(AXES, None), P(None, AXES)
    in_specs = (cols, rows, rows, cols, rows, rows, rows, cols, rows, rows, rows, rows, rows)
    step = functools.partial(body, (4, 8, 8))
    return jax.shard_map(step, mesh=split, in_specs=in_specs, out_specs=cols, check_vma=False)
```

time: 82.4 us -> 53.4 us (0.65)
  Pallas kernels: 82.2 us -> 53.2 us
    pallas_call x3 -> x1, Pallas kernels: 71.8 us -> 42.9 us  [mega(): pl.pallas_call(functools.partial(mega_kernel, dims), out_shape=(S((16, 32...]
where the time goes in v3:
time: 53.4 us; the launch traced here: 53.2 us
  Pallas kernels  53.2 us (100%)
    pallas_call x1, Pallas kernels, mega(): pl.pallas_call(functools.partial(mega_kernel, dims), out_shape=(S((16, 32...  42.9 us
    pallas_call x1, Pallas kernels, down(): pl.pallas_call(down_kernel, out_shape=S((16, 4096), F32), scratch_shapes=...  10.3 us

profile of v3, /device:TPU:1, one launch (start us, length us, event | category | flops | bytes accessed | tf_op | source)
XLA Modules:
  0.0 53.2 jit_solution(13650183083029260127)
XLA Ops:
  0.0 42.9 %shard_map.127 = (bf16[16,32]{1,0:T(8,128)(2,1)}, f32[512,32]{1,0:T(8,128)}) custom-call(f32[16,4096]{1,0:T(8,128)} %vec.1, s32[1,4096]{1,0:T(1,128)} %mor.3, s32[1,32]{1,0:T(1,128)} %siz.3, bf16[32,4096]{1,0:T(8,128)(2,1)} %bas.3, bf16[32,1024]{1,0:T(8,128)(2,1)} %lt.3, bf16[4,1024]{1,0:T(4,128)(2,1)} %mt.3, bf16[1,1024]{1,0:T(2,128)(2,1)} %rt.1, ...), custom_call_target="tpu_custom_call" | custom-call | tf_op jit(solution)/shard_map/pallas_call | solution.py:399
  42.9 10.3 %shard_map.128 = f32[16,4096]{1,0:T(8,128)} custom-call(bf16[16,32]{1,0:T(8,128)(2,1)} %get-tuple-element.7.top, f32[512,32]{1,0:T(8,128)} %get-tuple-element.8.far, s32[1,4096]{1,0:T(1,128)} %mor.3, s32[1,32]{1,0:T(1,128)} %siz.3, bf16[32,4096]{1,0:T(8,128)(2,1)} %bas.3, bf16[32,1024]{1,0:T(8,128)(2,1)} %lt.3, bf16[4,1024]{1,0:T(4,128)(2,1)} %mt.3), custom_call_target="tpu_custom_call" | custom-call | tf_op jit(solution)/shard_map/pallas_call | solution.py:96

commit v4 on v3

--- a/solution.py
+++ b/solution.py
@@ -47,10 +47,10 @@
     return jnp.sum(jnp.where(pos >= ends, 1.0, 0.0), axis=0, keepdims=True)
 
 
-CH = 256
-
-
-def down_kernel(top, far, mor, siz, bas, lt, mt, out, scat):
+CH = 1024
+
+
+def down_kernel(top, far, mor, siz, bas, lt, mt, out):
     erow, ecol = spread_row(), spread_col()
     back = hot(iota((1024, 32), 0) // 32 == iota((1024, 32), 1))
     xt = dot(top[...], ecol)
@@ -79,11 +79,10 @@
             o = jnp.where(leaf == l, wide[l * 16 : (l + 1) * 16], o)
         ob = o.astype(BF16)
         hib = jnp.broadcast_to(hi, (16, CH)).astype(F32).astype(BF16)
-        for h in range(16):
-            scat[h * 16 : (h + 1) * 16, :] = jnp.where(hib == h, ob, jnp.zeros((), BF16))
-        return acc + dot(scat[...], pick, NT)
-
-    acc = lax.fori_loop(0, 4096 // CH, chunk, jnp.zeros((256, 256), F32))
+        scat = jnp.concatenate([jnp.where(hib == h, ob, jnp.zeros((), BF16)) for h in range(16)], axis=0)
+        return acc + dot(scat, pick, NT)
+
+    acc = lax.fori_loop(0, 4096 // CH, chunk, jnp.zeros((256, 256), F32), unroll=2)
     for h in range(16):
         out[:, h * 256 : (h + 1) * 256] = acc[h * 16 : (h + 1) * 16]
 
@@ -93,8 +92,7 @@
 
 
 def down(top, far, mor, siz, bas, lt, mt):
-    return pl.pallas_call(down_kernel, out_shape=S((16, 4096), F32),
-        scratch_shapes=[VM((256, CH), BF16)])(top, far, mor, siz, bas, lt, mt)
+    return pl.pallas_call(down_kernel, out_shape=S((16, 4096), F32))(top, far, mor, siz, bas, lt, mt)
 
 
 AXES = ("leaf_0", "leaf_1", "leaf_2", "leaf_3")
@@ -146,6 +144,9 @@
     return dot(sel, hi, NT) + dot(sel, lo, NT)
 
 
+UP = 512
+
+
 def lanes_of(x):
     return x.reshape(x.shape[0], 512)
 
@@ -154,11 +155,20 @@
     return functools.reduce(lambda a, b: a + b, [t.astype(F32) for t in terms]).astype(BF16)
 
 
-def mega_kernel(dims, vec, mor, siz, bas, lt, mt, rt, pairs, lcoup, partner, dcoup, gpart, gcoup,
-                top_out, far_out,
+def mega_kernel(dims, *refs):
+    ins, (top_out, far_out), rest = refs[:13], refs[13:15], refs[15:]
+    staged, (inputs, *rest) = rest[:13], rest[13:]
+    mega_body(dims, ins, staged, inputs, top_out, far_out, *rest)
+
+
+def mega_body(dims, ins, staged, inputs, top_out, far_out,
                 masked, lt32, lc, s32, idcol, fwd, bwd,
                 ca, rsb, rx, sb, rx2, sb2, rr, gx, sgx, pgx, gcb, tb, gr2, tb2, gr, w,
                 rowb, termb, pgs, gcrow, send, recv):
+    loads = [pltpu.make_async_copy(a, b, inputs.at[i]) for i, (a, b) in enumerate(zip(ins, staged))]
+    for load in loads:
+        load.start()
+    vec, mor, siz, bas, lt, mt, rt, pairs, lcoup, partner, dcoup, gpart, gcoup = staged
     nx, ny, nz = dims
     halves = nz // 4
     plane, pgs_n = ny * nz, ny * halves
@@ -210,34 +220,38 @@
         def _():
             greet(mate(j))
 
+    for i in (0, 1, 2):
+        loads[i].wait()
+    vx = jnp.concatenate([vec[:, h * 256 : (h + 1) * 256] for h in range(16)], axis=0).astype(BF16)
+
+    def chunk(i, carry):
+        at = pl.multiple_of(i * UP, UP)
+        m = mor[:, pl.ds(at, UP)]
+        lo, hi = m & 255, m >> 8
+        wide = dot(vx, hot(iota((256, UP), 0) == lo))
+        hib = jnp.broadcast_to(hi, (16, UP))
+        sv = wide[0:16]
+        for h in range(1, 16):
+            sv = jnp.where(hib == h, wide[h * 16 : (h + 1) * 16], sv)
+        leaf = jnp.broadcast_to(leaf_of(siz, at, UP), (16, UP)).astype(BF16)
+        svb = sv.astype(BF16)
+        for l in range(32):
+            masked[l * 16 : (l + 1) * 16, pl.ds(at, UP)] = jnp.where(leaf == l, svb, jnp.zeros((), BF16))
+        return carry
+
+    lax.fori_loop(0, 4096 // UP, chunk, 0, unroll=2)
+    for load in loads[3:]:
+        load.wait()
     pgs[...] = jnp.zeros((1, 128), I32)
     pgs[:, 0:4] = gpart[...]
     lt32[...] = lt[...].astype(F32)
-    vx = jnp.concatenate([vec[:, h * 256 : (h + 1) * 256] for h in range(16)], axis=0).astype(BF16)
-
-    def chunk(i, carry):
-        at = pl.multiple_of(i * CH, CH)
-        m = mor[:, pl.ds(at, CH)]
-        lo, hi = m & 255, m >> 8
-        wide = dot(vx, hot(iota((256, CH), 0) == lo))
-        hib = jnp.broadcast_to(hi, (16, CH))
-        sv = wide[0:16]
-        for h in range(1, 16):
-            sv = jnp.where(hib == h, wide[h * 16 : (h + 1) * 16], sv)
-        leaf = jnp.broadcast_to(leaf_of(siz, at, CH), (16, CH)).astype(BF16)
-        svb = sv.astype(BF16)
-        for l in range(32):
-            masked[l * 16 : (l + 1) * 16, pl.ds(at, CH)] = jnp.where(leaf == l, svb, jnp.zeros((), BF16))
-        return carry
-
-    lax.fori_loop(0, 4096 // CH, chunk, 0)
-    lcv = dot(masked[...], bas[...], NT).astype(BF16)
+    lcv = dot(bas[...], masked[...], NT).astype(BF16)
     lc[...] = lcv
     erow, ecol = spread_row(), spread_col()
     root = jnp.zeros((16, 1024), F32)
     for m in range(4):
         acc = jnp.zeros((16, 1024), F32)
-        wide = dot(lcv[m * 128 : (m + 1) * 128], erow)
+        wide = dot(lcv[:, m * 128 : (m + 1) * 128], erow, TN)
         for l in range(8):
             acc = acc + wide[l * 16 : (l + 1) * 16] * lt32[m * 8 + l : m * 8 + l + 1, :]
         mid = fold_first(acc).astype(BF16)
@@ -269,6 +283,11 @@
         rsb[half] = dot(hotb, bk).astype(BF16).reshape(nx, plane, 4, 128)
     push(rsb.at[1 - c], rx, 4, sibling)
 
+    got(rx, 4)
+    sb[...] = add_all([rsb[c], rx[...]])
+    for j in range(1, nx):
+        push(sb.at[xs[j]], rx2.at[j - 1], 6, (xs[j], y, z, c))
+
     got(gx.at[pl.ds(0, 7)], 0)
     gcoef = sum_rows(gx, 8).astype(BF16)
     gcrow[...] = gcoef
@@ -289,11 +308,6 @@
     for j in range(1, nx):
         push(tb.at[xs[j]], gr2.at[j - 1], 7, (xs[j], y, z, c))
 
-    got(rx, 4)
-    sb[...] = add_all([rsb[c], rx[...]])
-    for j in range(1, nx):
-        push(sb.at[xs[j]], rx2.at[j - 1], 6, (xs[j], y, z, c))
-
     s32[...] = lcoup[...].astype(F32)
     each = hot(iota((64, 1024), 1) // 16 == iota((64, 1024), 0))
     pairsb = pairs[...].astype(F32).astype(BF16)
@@ -301,26 +315,26 @@
     back = hot(iota((1024, 32), 0) // 32 == iota((1024, 32), 1))
 
     def leaf_group(gi, carry):
-        at = pl.multiple_of(gi * 128, 128)
-        eye = iota((128, 512), 0) % 16 == iota((128, 512), 1) % 16
+        at = pl.multiple_of(gi * 256, 256)
+        eye = iota((256, 512), 0) % 16 == iota((256, 512), 1) % 16
         for which, e in ((1, ecol), (0, erow)):
-            leaf = jnp.broadcast_to(idcol[pl.ds(at, 128), which : which + 1], (128, 512))
-            chosen = dot(hot(eye & (leaf == (iota((128, 512), 1) // 16).astype(F32))), lc[...]).astype(BF16)
-            wide = dot(chosen, e)
-            parts = [wide[t * 16 : (t + 1) * 16] * s32[pl.ds(gi * 8 + t, 1), :] for t in range(8)]
+            leaf = jnp.broadcast_to(idcol[pl.ds(at, 256), which : which + 1], (256, 512))
+            here = hot(eye & (leaf == (iota((256, 512), 1) // 16).astype(F32)))
+            wide = dot(dot(here, lc[...], NT).astype(BF16), e)
+            parts = [wide[t * 16 : (t + 1) * 16] * s32[pl.ds(gi * 16 + t, 1), :] for t in range(16)]
             if which == 1:
                 out = dot(jnp.concatenate(parts, axis=0).astype(BF16), back)
-                fwd[pl.ds(at, 128), :] = out.astype(BF16)
+                fwd[pl.ds(at, 256), :] = out.astype(BF16)
             else:
                 out = jnp.concatenate([fold_first(t) for t in parts], axis=0)
-                bwd[pl.ds(at, 128), :] = out.astype(BF16)
+                bwd[pl.ds(at, 256), :] = out.astype(BF16)
         return carry
 
-    lax.fori_loop(0, 3, leaf_group, 0)
+    lax.fori_loop(0, 2, leaf_group, 0)
 
     got(ca.at[c, x, pl.ds(0, plane - 1)], 3)
     for j in range(1, nx):
-        push(ca.at[c, x], ca.at[c, x], 9, (xs[j], y, z, c))
+        push(ca.at[c, x], ca.at[c, x], 13 + j, (xs[j], y, z, c))
     push(ca.at[c, x], ca.at[c, x], 8, sibling)
 
     got(rx2, 6)
@@ -338,15 +352,19 @@
     for j in range(1, nx):
         push(gcb.at[x], gcb.at[x], 12, (xs[j], y, z, c))
 
-    lax.fori_loop(3, 8, leaf_group, 0)
-
-    got(ca.at[c, pl.ds(0, nx - 1)], 9)
-    for j in range(1, nx):
-        push(ca.at[c, xs[j]], ca.at[c, xs[j]], 13, sibling)
+    lax.fori_loop(2, 4, leaf_group, 0)
+
     ids = dot(pairsb, each)
     same = iota((512, 1024), 0) % 16 == iota((512, 1024), 1) % 16
     leaf = (iota((512, 1024), 0) // 16).astype(F32)
     far_out[...] = dot(hot(same & (leaf == ids[0:1])), fwd[...]) + dot(hot(same & (leaf == ids[1:2])), bwd[...])
+
+    for j in sorted(range(1, nx), key=lambda j: min(j, nx - j)):
+        got(ca.at[c, x], 13 + j)
+        push(ca.at[c, xs[-j]], ca.at[c, xs[-j]], 13, sibling)
+    got(gcb.at[pl.ds(0, nx - 1)], 12)
+    far = dot(hotg, lanes_of(gcb[...].reshape(groups, 4, 128)), TN).astype(BF16)
+    group_far = forward_sum(sg, far)
     got(ca.at[c, x], 8)
     got(ca.at[c, pl.ds(0, nx - 1)], 13)
     near = jnp.zeros((128, 512), F32)
@@ -355,9 +373,6 @@
         hotb = hot(ids == jnp.broadcast_to(partner[...], (chips, 128)))
         near = near + dot(hotb, lanes_of(ca[half].reshape(chips, 4, 128)), TN)
     root_far = forward_sum(dcoup[...], near.astype(BF16))
-    got(gcb.at[pl.ds(0, nx - 1)], 12)
-    far = dot(hotg, lanes_of(gcb[...].reshape(groups, 4, 128)), TN).astype(BF16)
-    group_far = forward_sum(sg, far)
 
     got(rr.at[pl.ds(0, plane - 1)], 10)
     root_far = root_far + unpack_row(sum_rows(rr, plane))
@@ -375,7 +390,8 @@
     sent(rx2, 6)
     sent(gr2, 7)
     sent(ca.at[c, x], 8)
-    sent(ca.at[c, pl.ds(0, nx - 1)], 9)
+    for j in range(1, nx):
+        sent(ca.at[c, x], 13 + j)
     sent(rr.at[pl.ds(0, plane - 1)], 10)
     sent(gr.at[pl.ds(0, pgs_n - 1)], 11)
     sent(gcb.at[pl.ds(0, nx - 1)], 12)
@@ -386,23 +402,23 @@
     nx, ny, nz = dims
     plane, pgn = ny * nz, ny * nz // 4
     b = lambda *s: pltpu.VMEM(s, BF16)
-    vm = pl.BlockSpec(memory_space=pltpu.VMEM)
+    ins = (vec, mor, siz, bas, lt, mt, rt, pairs, lcoup, partner, dcoup, gpart, gcoup)
     scratch = [
-        b(512, 4096), VM((32, 1024), F32), b(512, 32), VM((64, 1024), F32), VM((1024, 2), F32), b(1024, 32), b(1024, 32),
+        b(512, 4096), VM((32, 1024), F32), b(32, 512), VM((64, 1024), F32), VM((1024, 2), F32), b(1024, 32), b(1024, 32),
         b(2, nx, plane, 4, 128), b(2, nx, plane, 4, 128), b(nx, plane, 4, 128), b(nx, plane, 4, 128),
         b(nx - 1, plane, 4, 128), b(plane, 4, 128), b(plane, 4, 128),
         b(8, 4, 128), b(8, 4, 1024), VM((8, 1, 128), I32),
         b(nx, pgn, 4, 128), b(nx, pgn, 4, 128), b(nx - 1, pgn, 4, 128), b(pgn, 4, 128), b(pgn, 4, 128),
         b(1024, 512), b(4, 128), b(4, 128), VM((1, 128), I32), b(4, 128),
-        pltpu.SemaphoreType.DMA((14,)), pltpu.SemaphoreType.DMA((14,)),
+        pltpu.SemaphoreType.DMA((13 + nx,)), pltpu.SemaphoreType.DMA((13 + nx,)),
     ]
     return pl.pallas_call(
         functools.partial(mega_kernel, dims),
         out_shape=(S((16, 32), BF16), S((512, 32), F32)),
-        in_specs=[vm] * 13,
-        scratch_shapes=scratch,
+        in_specs=[pl.BlockSpec(memory_space=pl.ANY)] * 13,
+        scratch_shapes=[VM(a.shape, a.dtype) for a in ins] + [pltpu.SemaphoreType.DMA((13,))] + scratch,
         compiler_params=pltpu.CompilerParams(collective_id=0, has_side_effects=True),
-    )(vec, mor, siz, bas, lt, mt, rt, pairs, lcoup, partner, dcoup, gpart, gcoup)
+    )(*ins)
 
 
 def body(dims, vec, mor, siz, bas, lt, mt, rt, pairs, lcoup, partner, dcoup, gpart, gcoup):

time: 53.4 us -> 43.2 us (0.81)
  Pallas kernels: 53.2 us -> 43 us
    pallas_call x1, Pallas kernels: 42.9 us -> 37.6 us  [mega(): pl.pallas_call(functools.partial(mega_kernel, dims), out_shape=(S((16, 32...]
    pallas_call x1, Pallas kernels: 10.3 us -> 5.45 us  [down(): pl.pallas_call(down_kernel, out_shape=S((16, 4096), F32))]
where the time goes in v4:
time: 43.2 us; the launch traced here: 43 us
  Pallas kernels  43 us (100%)
    pallas_call x1, Pallas kernels, mega(): pl.pallas_call(functools.partial(mega_kernel, dims), out_shape=(S((16, 32...  37.6 us
    pallas_call x1, Pallas kernels, down(): pl.pallas_call(down_kernel, out_shape=S((16, 4096), F32))  5.45 us

profile of v4, /device:TPU:1, one launch (start us, length us, event | category | flops | bytes accessed | tf_op | source)
XLA Modules:
  0.0 43.0 jit_solution(10995054529480897588)
XLA Ops:
  0.0 37.6 %shard_map.127 = (bf16[16,32]{1,0:T(8,128)(2,1)}, f32[512,32]{1,0:T(8,128)}) custom-call(f32[16,4096]{1,0:T(8,128)} %refs_0_.1, s32[1,4096]{1,0:T(1,128)} %mor.1, s32[1,32]{1,0:T(1,128)} %siz.1, bf16[32,4096]{1,0:T(8,128)(2,1)} %bas.1, bf16[32,1024]{1,0:T(8,128)(2,1)} %lt.1, bf16[4,1024]{1,0:T(4,128)(2,1)} %mt.1, bf16[1,1024]{1,0:T(2,128)(2,1)} %refs_6_.1, ...), custom_call_target="tpu_custom_call" | custom-call | tf_op jit(solution)/shard_map/pallas_call | solution.py:415
  37.6 5.5 %shard_map.128 = f32[16,4096]{1,0:T(8,128)} custom-call(bf16[16,32]{1,0:T(8,128)(2,1)} %get-tuple-element.7.top, f32[512,32]{1,0:T(8,128)} %get-tuple-element.8.far, s32[1,4096]{1,0:T(1,128)} %mor.1, s32[1,32]{1,0:T(1,128)} %siz.1, bf16[32,4096]{1,0:T(8,128)(2,1)} %bas.1, bf16[32,1024]{1,0:T(8,128)(2,1)} %lt.1, bf16[4,1024]{1,0:T(4,128)(2,1)} %mt.1), custom_call_target="tpu_custom_call" | custom-call | tf_op jit(solution)/shard_map/pallas_call | solution.py:95

commit v5 on v4

--- a/solution.py
+++ b/solution.py
@@ -162,7 +162,7 @@
 
 
 def mega_body(dims, ins, staged, inputs, top_out, far_out,
-                masked, lt32, lc, s32, idcol, fwd, bwd,
+                masked, lt32, lc, s32, idcol, leaf_far,
                 ca, rsb, rx, sb, rx2, sb2, rr, gx, sgx, pgx, gcb, tb, gr2, tb2, gr, w,
                 rowb, termb, pgs, gcrow, send, recv):
     loads = [pltpu.make_async_copy(a, b, inputs.at[i]) for i, (a, b) in enumerate(zip(ins, staged))]
@@ -184,6 +184,9 @@
     far_first = lambda o: -(min(o[0], ny - o[0]) + min(o[1], nz - o[1]))
     offs = sorted([(a, b) for a in range(ny) for b in range(nz) if a or b], key=far_first)
     goffs = sorted([(a, b) for a in range(ny) for b in range(halves) if a or b], key=lambda o: -min(o[0], ny - o[0]))
+    near_y = [a for a in range(ny) if min(a, ny - a) <= ny // 4]
+    far_y = [a for a in range(ny) if a not in near_y]
+    row_of = lambda a: pl.ds(ys[a] * nz, nz)
     sibling = (x, y, z, 1 - c)
 
     def mate(j):
@@ -257,15 +260,15 @@
         mid = fold_first(acc).astype(BF16)
         root = root + dot(mid, erow) * mt[m : m + 1, :].astype(F32)
     root = fold_first(root).astype(BF16)
+    rowb[...] = pack_row(root).astype(BF16)
+    pl.semaphore_wait(bar, plane - 1 + nx - 1 + 4)
+
+    for a, b in offs:
+        push(rowb, ca.at[c, x, yz], 3 if a in near_y else 9, (x, ys[a], zs[b], c))
     term = fold_first(dot(root, erow) * rt[...].astype(F32)).astype(BF16)
     termb[...] = pack_row(term).astype(BF16)
-    rowb[...] = pack_row(root).astype(BF16)
-    pl.semaphore_wait(bar, plane - 1 + nx - 1 + 4)
-
     for j in range(1, 8):
         push(termb, gx.at[k], 0, mate(j))
-    for a, b in offs:
-        push(rowb, ca.at[c, x, yz], 3, (x, ys[a], zs[b], c))
     for j in range(1, 8):
         push(gcoup, sgx.at[k], 1, mate(j))
         push(pgs, pgx.at[k], 2, mate(j))
@@ -283,10 +286,34 @@
         rsb[half] = dot(hotb, bk).astype(BF16).reshape(nx, plane, 4, 128)
     push(rsb.at[1 - c], rx, 4, sibling)
 
+    s32[...] = lcoup[...].astype(F32)
+    back = hot(iota((1024, 32), 0) // 32 == iota((1024, 32), 1))
+    each = hot(iota((64, 1024), 1) // 16 == iota((64, 1024), 0))
+    idcol[...] = dot(each, pairs[...].astype(F32).astype(BF16), (((0,), (1,)), ((), ())))
+
+    def leaf_group(gi):
+        eye = iota((512, 512), 0) % 16 == iota((512, 512), 1) % 16
+        lid = (iota((512, 512), 1) // 16).astype(F32)
+        at = slice(gi * 512, gi * 512 + 512)
+        first, second = [
+            hot(eye & (jnp.broadcast_to(idcol[at, i : i + 1], (512, 512)) == lid)) for i in (0, 1)
+        ]
+        rows = [s32[gi * 32 + t : gi * 32 + t + 1, :] for t in range(32)]
+        wide = dot(dot(second, lc[...], NT).astype(BF16), ecol)
+        parts = [wide[t * 16 : (t + 1) * 16] * rows[t] for t in range(32)]
+        forth = dot(jnp.concatenate(parts, axis=0).astype(BF16), back).astype(BF16)
+        wide = dot(dot(first, lc[...], NT).astype(BF16), erow)
+        parts = [fold_first(wide[t * 16 : (t + 1) * 16] * rows[t]) for t in range(32)]
+        return dot(forth, first, TN) + dot(jnp.concatenate(parts, axis=0).astype(BF16), second, TN)
+
+    leaf_far[...] = leaf_group(0)
+
     got(rx, 4)
     sb[...] = add_all([rsb[c], rx[...]])
-    for j in range(1, nx):
-        push(sb.at[xs[j]], rx2.at[j - 1], 6, (xs[j], y, z, c))
+    for part, i in ((far_y, 6), (near_y, 13 + nx)):
+        for a in part:
+            for j in range(1, nx):
+                push(sb.at[xs[j], row_of(a)], rx2.at[j - 1, row_of(a)], i, (xs[j], y, z, c))
 
     got(gx.at[pl.ds(0, 7)], 0)
     gcoef = sum_rows(gx, 8).astype(BF16)
@@ -308,63 +335,43 @@
     for j in range(1, nx):
         push(tb.at[xs[j]], gr2.at[j - 1], 7, (xs[j], y, z, c))
 
-    s32[...] = lcoup[...].astype(F32)
-    each = hot(iota((64, 1024), 1) // 16 == iota((64, 1024), 0))
-    pairsb = pairs[...].astype(F32).astype(BF16)
-    idcol[...] = dot(each, pairsb, (((0,), (1,)), ((), ())))
-    back = hot(iota((1024, 32), 0) // 32 == iota((1024, 32), 1))
-
-    def leaf_group(gi, carry):
-        at = pl.multiple_of(gi * 256, 256)
-        eye = iota((256, 512), 0) % 16 == iota((256, 512), 1) % 16
-        for which, e in ((1, ecol), (0, erow)):
-            leaf = jnp.broadcast_to(idcol[pl.ds(at, 256), which : which + 1], (256, 512))
-            here = hot(eye & (leaf == (iota((256, 512), 1) // 16).astype(F32)))
-            wide = dot(dot(here, lc[...], NT).astype(BF16), e)
-            parts = [wide[t * 16 : (t + 1) * 16] * s32[pl.ds(gi * 16 + t, 1), :] for t in range(16)]
-            if which == 1:
-                out = dot(jnp.concatenate(parts, axis=0).astype(BF16), back)
-                fwd[pl.ds(at, 256), :] = out.astype(BF16)
-            else:
-                out = jnp.concatenate([fold_first(t) for t in parts], axis=0)
-                bwd[pl.ds(at, 256), :] = out.astype(BF16)
-        return carry
-
-    lax.fori_loop(0, 2, leaf_group, 0)
-
-    got(ca.at[c, x, pl.ds(0, plane - 1)], 3)
-    for j in range(1, nx):
-        push(ca.at[c, x], ca.at[c, x], 13 + j, (xs[j], y, z, c))
+    def along_x(part):
+        for a in part:
+            for j in range(1, nx):
+                push(ca.at[c, x, row_of(a)], ca.at[c, x, row_of(a)], 13 + j, (xs[j], y, z, c))
+
+    got(ca.at[c, x, pl.ds(0, len(near_y) * nz - 1)], 3)
+    along_x(near_y)
+    got(ca.at[c, x, pl.ds(0, len(far_y) * nz)], 9)
+    along_x(far_y)
     push(ca.at[c, x], ca.at[c, x], 8, sibling)
 
-    got(rx2, 6)
-    sb2[...] = add_all([sb[x]] + [rx2[j] for j in range(nx - 1)])
-    for a, b in offs:
-        push(sb2.at[ys[a] * nz + zs[b]], rr.at[yz], 10, (x, ys[a], zs[b], c))
-    rr[yz] = sb2[yz]
+    def over_plane(part, i):
+        got(rx2.at[:, pl.ds(0, len(part) * nz)], i)
+        for a in part:
+            sb2[row_of(a)] = add_all([sb[x, row_of(a)]] + [rx2[j, row_of(a)] for j in range(nx - 1)])
+        for a, b in offs:
+            if a in part:
+                push(sb2.at[ys[a] * nz + zs[b]], rr.at[yz], 10, (x, ys[a], zs[b], c))
+
+    over_plane(far_y, 6)
     got(gr2, 7)
     tb2[...] = add_all([tb[x]] + [gr2[j] for j in range(nx - 1)])
     for a, b in goffs:
         push(tb2.at[ys[a] * halves + (zh + b) % halves], gr.at[pg], 11, (x, ys[a], gz[b], c))
     gr[pg] = tb2[pg]
-
+    over_plane(near_y, 13 + nx)
+    rr[yz] = sb2[yz]
+
+    leaf_far[...] += leaf_group(1)
+
+    for j in sorted(range(1, nx), key=lambda j: min(j, nx - j)):
+        got(ca.at[c, x], 13 + j)
+        push(ca.at[c, xs[-j]], ca.at[c, xs[-j]], 13, sibling)
     got(gcb.at[x, pl.ds(0, pgs_n - 1)], 5)
     for j in range(1, nx):
         push(gcb.at[x], gcb.at[x], 12, (xs[j], y, z, c))
-
-    lax.fori_loop(2, 4, leaf_group, 0)
-
-    ids = dot(pairsb, each)
-    same = iota((512, 1024), 0) % 16 == iota((512, 1024), 1) % 16
-    leaf = (iota((512, 1024), 0) // 16).astype(F32)
-    far_out[...] = dot(hot(same & (leaf == ids[0:1])), fwd[...]) + dot(hot(same & (leaf == ids[1:2])), bwd[...])
-
-    for j in sorted(range(1, nx), key=lambda j: min(j, nx - j)):
-        got(ca.at[c, x], 13 + j)
-        push(ca.at[c, xs[-j]], ca.at[c, xs[-j]], 13, sibling)
-    got(gcb.at[pl.ds(0, nx - 1)], 12)
-    far = dot(hotg, lanes_of(gcb[...].reshape(groups, 4, 128)), TN).astype(BF16)
-    group_far = forward_sum(sg, far)
+    far_out[...] = leaf_far[...].T
     got(ca.at[c, x], 8)
     got(ca.at[c, pl.ds(0, nx - 1)], 13)
     near = jnp.zeros((128, 512), F32)
@@ -373,21 +380,25 @@
         hotb = hot(ids == jnp.broadcast_to(partner[...], (chips, 128)))
         near = near + dot(hotb, lanes_of(ca[half].reshape(chips, 4, 128)), TN)
     root_far = forward_sum(dcoup[...], near.astype(BF16))
-
+    got(gcb.at[pl.ds(0, nx - 1)], 12)
+    far = dot(hotg, lanes_of(gcb[...].reshape(groups, 4, 128)), TN).astype(BF16)
+    group_far = forward_sum(sg, far)
+    got(gr.at[pl.ds(0, pgs_n - 1)], 11)
+    group_far = (group_far + unpack_row(sum_rows(gr, pgs_n))).astype(BF16)
     got(rr.at[pl.ds(0, plane - 1)], 10)
     root_far = root_far + unpack_row(sum_rows(rr, plane))
-    got(gr.at[pl.ds(0, pgs_n - 1)], 11)
-    group_far = (group_far + unpack_row(sum_rows(gr, pgs_n))).astype(BF16)
     hi, lo = split2(dot(group_far, ecol) * rt[...].astype(F32))
     top_out[...] = (root_far + dot(hi, back) + dot(lo, back)).astype(BF16)
 
     sent(gx.at[pl.ds(0, 7)], 0)
     sent(sgx.at[pl.ds(0, 7)], 1)
     sent(pgx.at[pl.ds(0, 7)], 2)
-    sent(ca.at[c, x, pl.ds(0, plane - 1)], 3)
+    sent(ca.at[c, x, pl.ds(0, len(near_y) * nz - 1)], 3)
+    sent(ca.at[c, x, pl.ds(0, len(far_y) * nz)], 9)
     sent(rx, 4)
     sent(gcb.at[x, pl.ds(0, pgs_n - 1)], 5)
-    sent(rx2, 6)
+    sent(rx2.at[:, pl.ds(0, len(far_y) * nz)], 6)
+    sent(rx2.at[:, pl.ds(0, len(near_y) * nz)], 13 + nx)
     sent(gr2, 7)
     sent(ca.at[c, x], 8)
     for j in range(1, nx):
@@ -404,13 +415,13 @@
     b = lambda *s: pltpu.VMEM(s, BF16)
     ins = (vec, mor, siz, bas, lt, mt, rt, pairs, lcoup, partner, dcoup, gpart, gcoup)
     scratch = [
-        b(512, 4096), VM((32, 1024), F32), b(32, 512), VM((64, 1024), F32), VM((1024, 2), F32), b(1024, 32), b(1024, 32),
+        b(512, 4096), VM((32, 1024), F32), b(32, 512), VM((64, 1024), F32), VM((1024, 2), F32), VM((32, 512), F32),
         b(2, nx, plane, 4, 128), b(2, nx, plane, 4, 128), b(nx, plane, 4, 128), b(nx, plane, 4, 128),
         b(nx - 1, plane, 4, 128), b(plane, 4, 128), b(plane, 4, 128),
         b(8, 4, 128), b(8, 4, 1024), VM((8, 1, 128), I32),
         b(nx, pgn, 4, 128), b(nx, pgn, 4, 128), b(nx - 1, pgn, 4, 128), b(pgn, 4, 128), b(pgn, 4, 128),
         b(1024, 512), b(4, 128), b(4, 128), VM((1, 128), I32), b(4, 128),
-        pltpu.SemaphoreType.DMA((13 + nx,)), pltpu.SemaphoreType.DMA((13 + nx,)),
+        pltpu.SemaphoreType.DMA((14 + nx,)), pltpu.SemaphoreType.DMA((14 + nx,)),
     ]
     return pl.pallas_call(
         functools.partial(mega_kernel, dims),

time: 43.2 us -> 41.8 us (0.968)
  Pallas kernels: 43 us -> 41.6 us
    pallas_call x1, Pallas kernels: 37.6 us -> 36.2 us  [mega(): pl.pallas_call(functools.partial(mega_kernel, dims), out_shape=(S((16, 32...]
where the time goes in v5:
time: 41.8 us; the launch traced here: 41.6 us
  Pallas kernels  41.6 us (100%)
    pallas_call x1, Pallas kernels, mega(): pl.pallas_call(functools.partial(mega_kernel, dims), out_shape=(S((16, 32...  36.2 us
    pallas_call x1, Pallas kernels, down(): pl.pallas_call(down_kernel, out_shape=S((16, 4096), F32))  5.45 us

profile of v5, /device:TPU:1, one launch (start us, length us, event | category | flops | bytes accessed | tf_op | source)
XLA Modules:
  0.0 41.6 jit_solution(4284806526867074764)
XLA Ops:
  0.0 36.2 %shard_map.127 = (bf16[16,32]{1,0:T(8,128)(2,1)}, f32[512,32]{1,0:T(8,128)}) custom-call(f32[16,4096]{1,0:T(8,128)} %refs_0_.1, s32[1,4096]{1,0:T(1,128)} %mor.1, s32[1,32]{1,0:T(1,128)} %siz.1, bf16[32,4096]{1,0:T(8,128)(2,1)} %bas.1, bf16[32,1024]{1,0:T(8,128)(2,1)} %lt.1, bf16[4,1024]{1,0:T(4,128)(2,1)} %mt.1, bf16[1,1024]{1,0:T(2,128)(2,1)} %refs_6_.1, ...), custom_call_target="tpu_custom_call" | custom-call | tf_op jit(solution)/shard_map/pallas_call | solution.py:426
  36.2 5.5 %shard_map.128 = f32[16,4096]{1,0:T(8,128)} custom-call(bf16[16,32]{1,0:T(8,128)(2,1)} %get-tuple-element.7.top, f32[512,32]{1,0:T(8,128)} %get-tuple-element.8.far, s32[1,4096]{1,0:T(1,128)} %mor.1, s32[1,32]{1,0:T(1,128)} %siz.1, bf16[32,4096]{1,0:T(8,128)(2,1)} %bas.1, bf16[32,1024]{1,0:T(8,128)(2,1)} %lt.1, bf16[4,1024]{1,0:T(4,128)(2,1)} %mt.1), custom_call_target="tpu_custom_call" | custom-call | tf_op jit(solution)/shard_map/pallas_call | solution.py:95

commit v6 on v5

--- a/solution.py
+++ b/solution.py
@@ -260,15 +260,15 @@
         mid = fold_first(acc).astype(BF16)
         root = root + dot(mid, erow) * mt[m : m + 1, :].astype(F32)
     root = fold_first(root).astype(BF16)
+    term = fold_first(dot(root, erow) * rt[...].astype(F32)).astype(BF16)
     rowb[...] = pack_row(root).astype(BF16)
+    termb[...] = pack_row(term).astype(BF16)
     pl.semaphore_wait(bar, plane - 1 + nx - 1 + 4)
 
+    for j in range(1, 8):
+        push(termb, gx.at[k], 0, mate(j))
     for a, b in offs:
         push(rowb, ca.at[c, x, yz], 3 if a in near_y else 9, (x, ys[a], zs[b], c))
-    term = fold_first(dot(root, erow) * rt[...].astype(F32)).astype(BF16)
-    termb[...] = pack_row(term).astype(BF16)
-    for j in range(1, 8):
-        push(termb, gx.at[k], 0, mate(j))
     for j in range(1, 8):
         push(gcoup, sgx.at[k], 1, mate(j))
         push(pgs, pgx.at[k], 2, mate(j))
@@ -308,20 +308,6 @@
 
     leaf_far[...] = leaf_group(0)
 
-    got(rx, 4)
-    sb[...] = add_all([rsb[c], rx[...]])
-    for part, i in ((far_y, 6), (near_y, 13 + nx)):
-        for a in part:
-            for j in range(1, nx):
-                push(sb.at[xs[j], row_of(a)], rx2.at[j - 1, row_of(a)], i, (xs[j], y, z, c))
-
-    got(gx.at[pl.ds(0, 7)], 0)
-    gcoef = sum_rows(gx, 8).astype(BF16)
-    gcrow[...] = gcoef
-    for a, b in goffs:
-        push(gcrow, gcb.at[x, pg], 5, (x, ys[a], gz[b], c))
-    gcb[x, pg] = gcoef
-
     got(sgx.at[pl.ds(0, 7)], 1)
     got(pgx.at[pl.ds(0, 7)], 2)
     sg = sgx[...].reshape(32, 1024)
@@ -330,6 +316,21 @@
     spread = dot(p8, hot(iota((4, 32), 1) % 4 == iota((4, 32), 0)))
     gpair = jnp.sum(jnp.where(iota((8, 32), 1) // 4 == iota((8, 32), 0), spread, 0.0), axis=0, keepdims=True)
     hotg = hot(iota((groups, 32), 0).astype(F32) == jnp.broadcast_to(gpair, (groups, 32)))
+
+    got(rx, 4)
+    sb[...] = add_all([rsb[c], rx[...]])
+    for part, i in ((far_y, 6), (near_y, 13 + nx)):
+        for a in part:
+            for j in range(1, nx):
+                push(sb.at[xs[j], row_of(a)], rx2.at[j - 1, row_of(a)], i, (xs[j], y, z, c))
+
+    got(gx.at[pl.ds(0, 7)], 0)
+    gcoef = sum_rows(gx, 8).astype(BF16)
+    gcrow[...] = gcoef
+    for a, b in goffs:
+        push(gcrow, gcb.at[x, pg], 5, (x, ys[a], gz[b], c))
+    gcb[x, pg] = gcoef
+
     back_weights(unpack_row(gcoef.astype(F32)).astype(BF16), w)
     tb[...] = dot(hotg, dot(sg, w[...]).astype(BF16)).astype(BF16).reshape(nx, pgs_n, 4, 128)
     for j in range(1, nx):

time: 41.8 us -> 43.9 us (1.050)
  Pallas kernels: 41.6 us -> 43.8 us
    pallas_call x1, Pallas kernels: 36.2 us -> 38.3 us  [mega(): pl.pallas_call(functools.partial(mega_kernel, dims), out_shape=(S((16, 32...]
where the time goes in v6:
time: 43.9 us; the launch traced here: 43.8 us
  Pallas kernels  43.8 us (100%)
    pallas_call x1, Pallas kernels, mega(): pl.pallas_call(functools.partial(mega_kernel, dims), out_shape=(S((16, 32...  38.3 us
    pallas_call x1, Pallas kernels, down(): pl.pallas_call(down_kernel, out_shape=S((16, 4096), F32))  5.45 us

profile of v6, /device:TPU:1, one launch (start us, length us, event | category | flops | bytes accessed | tf_op | source)
XLA Modules:
  0.0 43.8 jit_solution(121660475636711807)
XLA Ops:
  0.0 38.3 %shard_map.127 = (bf16[16,32]{1,0:T(8,128)(2,1)}, f32[512,32]{1,0:T(8,128)}) custom-call(f32[16,4096]{1,0:T(8,128)} %refs_0_.1, s32[1,4096]{1,0:T(1,128)} %mor.1, s32[1,32]{1,0:T(1,128)} %siz.1, bf16[32,4096]{1,0:T(8,128)(2,1)} %bas.1, bf16[32,1024]{1,0:T(8,128)(2,1)} %lt.1, bf16[4,1024]{1,0:T(4,128)(2,1)} %mt.1, bf16[1,1024]{1,0:T(2,128)(2,1)} %refs_6_.1, ...), custom_call_target="tpu_custom_call" | custom-call | tf_op jit(solution)/shard_map/pallas_call | solution.py:427
  38.3 5.4 %shard_map.128 = f32[16,4096]{1,0:T(8,128)} custom-call(bf16[16,32]{1,0:T(8,128)(2,1)} %get-tuple-element.7.top, f32[512,32]{1,0:T(8,128)} %get-tuple-element.8.far, s32[1,4096]{1,0:T(1,128)} %mor.1, s32[1,32]{1,0:T(1,128)} %siz.1, bf16[32,4096]{1,0:T(8,128)(2,1)} %bas.1, bf16[32,1024]{1,0:T(8,128)(2,1)} %lt.1, bf16[4,1024]{1,0:T(4,128)(2,1)} %mt.1), custom_call_target="tpu_custom_call" | custom-call | tf_op jit(solution)/shard_map/pallas_call | solution.py:95

commit v7 on v5

--- a/solution.py
+++ b/solution.py
@@ -47,7 +47,7 @@
     return jnp.sum(jnp.where(pos >= ends, 1.0, 0.0), axis=0, keepdims=True)
 
 
-CH = 1024
+CH = 4096
 
 
 def down_kernel(top, far, mor, siz, bas, lt, mt, out):
@@ -260,18 +260,18 @@
         mid = fold_first(acc).astype(BF16)
         root = root + dot(mid, erow) * mt[m : m + 1, :].astype(F32)
     root = fold_first(root).astype(BF16)
+    term = fold_first(dot(root, erow) * rt[...].astype(F32)).astype(BF16)
     rowb[...] = pack_row(root).astype(BF16)
+    termb[...] = pack_row(term).astype(BF16)
     pl.semaphore_wait(bar, plane - 1 + nx - 1 + 4)
 
-    for a, b in offs:
-        push(rowb, ca.at[c, x, yz], 3 if a in near_y else 9, (x, ys[a], zs[b], c))
-    term = fold_first(dot(root, erow) * rt[...].astype(F32)).astype(BF16)
-    termb[...] = pack_row(term).astype(BF16)
     for j in range(1, 8):
         push(termb, gx.at[k], 0, mate(j))
     for j in range(1, 8):
         push(gcoup, sgx.at[k], 1, mate(j))
         push(pgs, pgx.at[k], 2, mate(j))
+    for a, b in offs:
+        push(rowb, ca.at[c, x, yz], 3 if a in near_y else 9, (x, ys[a], zs[b], c))
     gx[k] = termb[...]
     sgx[k] = gcoup[...]
     pgx[k] = pgs[...]
@@ -330,6 +330,7 @@
     spread = dot(p8, hot(iota((4, 32), 1) % 4 == iota((4, 32), 0)))
     gpair = jnp.sum(jnp.where(iota((8, 32), 1) // 4 == iota((8, 32), 0), spread, 0.0), axis=0, keepdims=True)
     hotg = hot(iota((groups, 32), 0).astype(F32) == jnp.broadcast_to(gpair, (groups, 32)))
+
     back_weights(unpack_row(gcoef.astype(F32)).astype(BF16), w)
     tb[...] = dot(hotg, dot(sg, w[...]).astype(BF16)).astype(BF16).reshape(nx, pgs_n, 4, 128)
     for j in range(1, nx):

time: 41.8 us -> 41 us (0.981)
  Pallas kernels: 41.6 us -> 40.9 us
    pallas_call x1, Pallas kernels: 5.45 us -> 4.92 us  [down(): pl.pallas_call(down_kernel, out_shape=S((16, 4096), F32))]
where the time goes in v7:
time: 41 us; the launch traced here: 40.9 us
  Pallas kernels  40.9 us (100%)
    pallas_call x1, Pallas kernels, mega(): pl.pallas_call(functools.partial(mega_kernel, dims), out_shape=(S((16, 32...  35.9 us
    pallas_call x1, Pallas kernels, down(): pl.pallas_call(down_kernel, out_shape=S((16, 4096), F32))  4.92 us

profile of v7, /device:TPU:1, one launch (start us, length us, event | category | flops | bytes accessed | tf_op | source)
XLA Modules:
  0.0 40.9 jit_solution(4302662257458606287)
XLA Ops:
  0.0 35.9 %shard_map.127 = (bf16[16,32]{1,0:T(8,128)(2,1)}, f32[512,32]{1,0:T(8,128)}) custom-call(f32[16,4096]{1,0:T(8,128)} %refs_0_.1, s32[1,4096]{1,0:T(1,128)} %mor.1, s32[1,32]{1,0:T(1,128)} %siz.1, bf16[32,4096]{1,0:T(8,128)(2,1)} %bas.1, bf16[32,1024]{1,0:T(8,128)(2,1)} %lt.1, bf16[4,1024]{1,0:T(4,128)(2,1)} %mt.1, bf16[1,1024]{1,0:T(2,128)(2,1)} %refs_6_.1, ...), custom_call_target="tpu_custom_call" | custom-call | tf_op jit(solution)/shard_map/pallas_call | solution.py:427
  35.9 4.9 %shard_map.128 = f32[16,4096]{1,0:T(8,128)} custom-call(bf16[16,32]{1,0:T(8,128)(2,1)} %get-tuple-element.7.top, f32[512,32]{1,0:T(8,128)} %get-tuple-element.8.far, s32[1,4096]{1,0:T(1,128)} %mor.1, s32[1,32]{1,0:T(1,128)} %siz.1, bf16[32,4096]{1,0:T(8,128)(2,1)} %bas.1, bf16[32,1024]{1,0:T(8,128)(2,1)} %lt.1, bf16[4,1024]{1,0:T(4,128)(2,1)} %mt.1), custom_call_target="tpu_custom_call" | custom-call | tf_op jit(solution)/shard_map/pallas_call | solution.py:95
